TPU v7x, 128 devices: a whole 4x4x4 slice. The times are simulated.
128 devices in a mesh: mx: 8 (over x, core), my: 8 (over y, z_lo), mz: 2 (over z_hi).
Axes of the slice: x: 4, y: 4, z: 4 (z_hi: 2, z_lo: 2; z = z_hi * 2 + z_lo), core: 2. Of those that a mesh axis runs over, the one named last changes fastest.
Arguments:
- force: float32 [3, 128, 256, 256], P(None, 'mx', 'my', 'mz'), may hold values from -6 to 6
- velocity_prev: float32 [3, 128, 256, 256], P(None, 'mx', 'my', 'mz'), may hold values from -2 to 2
- viscosity: float32 [128, 256, 256], P('mx', 'my', 'mz'), may hold values from 0.5 to 8
- strain: float32 [128, 256, 256], P('mx', 'my', 'mz'), may hold values from 0 to 2
- yield_flags: int32 [128, 256, 256], P('mx', 'my', 'mz'), may hold values 0 or 1
- counts: int32 [2], replicated, may hold values from 4 to 6, as said below
- heights: float32 [128, 256], P('mx'), may hold values from 0 to 2
- receivers: int32 [128, 256], P('mx'), may hold values from 0 to 7
Outputs:
- velocity: float32 [3, 128, 256, 256], P(None, 'mx', 'my', 'mz')
- strain_out: float32 [128, 256, 256], P('mx', 'my', 'mz')
- topography: float32 [128, 256], P('mx')
Inputs may be any that keep to these rules, and one draw needn't show every extreme that they name: `counts`: some Picard iteration takes 6 Krylov iterations and another takes 6 - 2.
All inputs are finite; a program needn't handle non-finite values. No bound on the sum of `yield_flags` on one device may be relied on, other than what follows from the above.
Results may differ from a plain program's by a relative error of at most 0.0003.
Values sent between devices are 32-bit elements; how exact they have to be, the bound alone decides.
A program may use at most 128 MiB of HBM per device.

v0:
```python
import functools
import math

import jax
import jax.numpy as jnp
from jax import lax
from jax.sharding import Mesh
from jax.sharding import PartitionSpec as P

PICARD = 2
KMAX = 6
SWEEPS = 4
MX_MY_MZ = ("mx_0", "mx_1", "my_0", "my_1", "mz")
MX = ("mx_0", "mx_1")
MY = ("my_0", "my_1")
MY_MZ = ("my_0", "my_1", "mz")


drag_coef = 0.05
cohesion_base = 1.0
weakening = 0.6
critical_strain = 1.0
sin_friction = 0.5
cos_friction = 0.8660254
pressure_gradient = 2.0
rate_floor = 0.1
strain_step = 0.5
uplift_gain = 8.0
surface_step = 0.2
erodibility = 0.5
neighbour_steps = ((-1, -1), (-1, 0), (-1, 1), (0, -1), (0, 1), (1, -1), (1, 0), (1, 1))


def with_halo(array, sides, width):
    edges = {}
    for axis, dim in sides:
        peers, length = (lax.axis_size(axis), array.shape[dim])
        up = [(i, (i + 1) % peers) for i in range(peers - 1)]
        last = lax.slice_in_dim(array, length - width, length, axis=dim)
        initial = lax.slice_in_dim(array, 0, width, axis=dim)
        edges[dim] = (
            lax.ppermute(last, axis, up),
            lax.ppermute(initial, axis, [(b, a) for a, b in up]),
        )
    done = []
    for _, dim in sides:
        low, high = edges[dim]
        around = [(width, width) if d in done else (0, 0) for d in range(array.ndim)]
        array = jnp.concatenate([jnp.pad(low, around), array, jnp.pad(high, around)], axis=dim)
        done.append(dim)
    return array


def extended(array, sides, width):
    for axis, dim in sides:
        peers, length = (lax.axis_size(axis), array.shape[dim])
        up = [(i, (i + 1) % peers) for i in range(peers - 1)]
        down = [(j, i) for i, j in up]
        last = lax.slice_in_dim(array, length - width, length, axis=dim)
        initial = lax.slice_in_dim(array, 0, width, axis=dim)
        before = lax.ppermute(last, axis, up)
        after = lax.ppermute(initial, axis, down)
        array = jnp.concatenate([before, array, after], axis=dim)
    return array


def by_axis(array, axes):
    return functools.reduce(lax.psum, axes, array)


def copy_for_each(array, axis):
    peers = lax.axis_size(axis)
    return lax.all_to_all(
        jnp.broadcast_to(array[None], (peers, *array.shape)), axis, 0, 0, tiled=True
    )


def in_order(tiles, dim):
    tiles = jnp.moveaxis(tiles, 0, dim)
    shape = tiles.shape
    return tiles.reshape(*shape[:dim], shape[dim] * shape[dim + 1], *shape[dim + 2 :])


def gather_directly(array, axis, dim):
    tiles = copy_for_each(array, axis)
    return in_order(tiles, dim)


def neighbour(padded, dimension, offset):
    window = [slice(None), slice(1, -1), slice(1, -1), slice(1, -1)]
    window[dimension + 1] = slice(1 + offset, padded.shape[dimension + 1] - 1 + offset)
    return padded[tuple(window)]


def face_rims(field):
    return with_halo(field, ((MX, 1), (MY, 2), ("mz", 3)), 1)


def material_rims(stacked):
    return extended(stacked, ((MX, 1), (MY, 2), ("mz", 3)), 1)


def deep_rims(field):
    return extended(field, ((MX, 1), (MY, 2), ("mz", 3)), 2)


def row_rims(block):
    return extended(block, ((MX, 0),), 1)


def paired_products(residual, applied):
    return (
        by_axis(jnp.sum(residual * residual), MX_MY_MZ),
        by_axis(jnp.sum(residual * applied), MX_MY_MZ),
    )


def apply_padded(padded, eta_padded):
    centre = padded[:, 1:-1, 1:-1, 1:-1]
    eta_centre = eta_padded[:, 1:-1, 1:-1, 1:-1]
    summed = drag_coef * centre
    for dimension in range(3):
        for offset in (-1, 1):
            face_eta = 0.5 * (eta_centre + neighbour(eta_padded, dimension, offset))
            summed = summed + face_eta * (centre - neighbour(padded, dimension, offset))
    return summed


def rate_invariant(padded):
    gradients = [
        0.5 * (neighbour(padded, dimension, 1) - neighbour(padded, dimension, -1))
        for dimension in range(3)
    ]
    summed = jnp.zeros_like(gradients[0][0])
    for outer_axis in range(3):
        for inner_axis in range(3):
            tensor = 0.5 * (gradients[inner_axis][outer_axis] + gradients[outer_axis][inner_axis])
            summed = summed + tensor * tensor
    return jnp.sqrt(0.5 * summed)


def yield_strength(strain, yield_flags, pressure):
    weakened = yield_flags.astype(jnp.float32) * jnp.minimum(strain / critical_strain, 1.0)
    return cohesion_base * (1.0 - weakening * weakened) * cos_friction + pressure * sin_friction


def viscosity_of(strain_rate, viscosity, strength):
    return jnp.minimum(viscosity, strength / (2.0 * jnp.maximum(strain_rate, rate_floor)))


def inside_mask(position, extent, cells):
    spots = position * cells + jnp.arange(-1, cells + 1, dtype=jnp.int32)
    return ((spots >= 0) & (spots < extent * cells)).astype(jnp.float32)


def spread_area(drained, receivers):
    summed = jnp.zeros((drained.shape[0] + 2, drained.shape[1] + 2), drained.dtype)
    for direction, (row_step, col_step) in enumerate(neighbour_steps):
        outflow = jnp.where(receivers == direction, drained, 0.0)
        summed = summed + jnp.pad(
            outflow, ((1 + row_step, 1 - row_step), (1 + col_step, 1 - col_step))
        )
    return summed


def finish_topography(heights, padded, receivers, drained, uplift):
    row_count, col_count = heights.shape
    receiver_height = jnp.zeros_like(heights)
    spacing = jnp.zeros_like(heights)
    for direction, (row_step, col_step) in enumerate(neighbour_steps):
        chosen = receivers == direction
        shifted = padded[
            1 + row_step : 1 + row_step + row_count, 1 + col_step : 1 + col_step + col_count
        ]
        receiver_height = receiver_height + jnp.where(chosen, shifted, 0.0)
        spacing = spacing + jnp.where(
            chosen, math.sqrt(row_step * row_step + col_step * col_step), 0.0
        )
    gradient = jnp.maximum(heights - receiver_height, 0.0) / spacing
    return heights + surface_step * (
        uplift_gain * uplift - erodibility * jnp.sqrt(drained) * gradient
    )


def krylov_solve(padded_start, start, force, eta_padded, iteration_limit):

    def operate(field):
        return apply_padded(face_rims(field), eta_padded)

    residual = force - apply_padded(padded_start, eta_padded)
    solution = start
    applied = operate(residual)
    current, product = paired_products(residual, applied)
    step_size = current / product
    beta_ratio = jnp.zeros_like(current)
    direction = jnp.zeros_like(residual)
    along_applied = jnp.zeros_like(residual)
    for iteration in range(KMAX):
        active = iteration < iteration_limit
        direction = residual + beta_ratio * direction
        along_applied = applied + beta_ratio * along_applied
        stepped = jnp.where(active, step_size, 0.0)
        solution = solution + stepped * direction
        residual = residual - stepped * along_applied
        if iteration + 1 < KMAX:
            applied = operate(residual)
            updated, product = paired_products(residual, applied)
            next_ratio = updated / current
            next_step = updated / (product - next_ratio * updated / step_size)
            step_size = jnp.where(active, next_step, step_size)
            beta_ratio = jnp.where(active, next_ratio, beta_ratio)
            current = jnp.where(active, updated, current)
    return solution


def local(force, velocity_prev, viscosity, strain, yield_flags, counts, heights, receivers):
    depth_cells = viscosity.shape[2]
    layers = lax.axis_size("mz") * depth_cells
    levels = lax.axis_index("mz") * depth_cells + jnp.arange(depth_cells, dtype=jnp.int32)
    pressure = pressure_gradient * (layers - 0.5 - levels.astype(jnp.float32)) / layers
    strength = yield_strength(strain, yield_flags, pressure)
    velocity = velocity_prev
    material = material_rims(jnp.stack([viscosity, strength]))
    inside = (
        inside_mask(lax.axis_index(MX), lax.axis_size(MX), viscosity.shape[0])[:, None, None]
        * inside_mask(lax.axis_index(MY), lax.axis_size(MY), viscosity.shape[1])[None, :, None]
        * inside_mask(lax.axis_index("mz"), lax.axis_size("mz"), viscosity.shape[2])[None, None, :]
    )
    for picard_index in range(PICARD):
        deep = deep_rims(velocity)
        widened = viscosity_of(rate_invariant(deep), material[0], material[1]) * inside
        padded = deep[:, 1:-1, 1:-1, 1:-1]
        velocity = krylov_solve(padded, velocity, force, widened[None], counts[picard_index])
    padded = face_rims(velocity)
    plastic = jnp.maximum(rate_invariant(padded) - strength / (2.0 * viscosity), 0.0)
    strain_out = strain + strain_step * plastic
    column = jnp.sum(velocity[2], axis=-1)
    gathered = gather_directly(column, MY_MZ, 1)
    row_count = column.shape[0]
    tiles_across = lax.axis_size(MY)
    tiles_depth = lax.axis_size("mz")
    columns_dev = column.shape[1]
    uplift = gathered.reshape(row_count, tiles_across, tiles_depth, columns_dev).sum(axis=2)
    uplift = uplift.reshape(row_count, tiles_across * columns_dev) / layers
    drained = jnp.ones_like(heights)
    for sweep_index in range(SWEEPS):
        spread = spread_area(drained, receivers)
        edges = jnp.stack([spread[0, 1:-1], spread[-1, 1:-1]])
        arrived = row_rims(edges)
        interior = spread[1:-1, 1:-1]
        interior = interior.at[0].add(arrived[0]).at[-1].add(arrived[3])
        drained = 1.0 + interior
    height_padded = jnp.pad(row_rims(heights), ((0, 0), (1, 1)))
    topography = finish_topography(heights, height_padded, receivers, drained, uplift)
    return (velocity, strain_out, topography)


def solution(mesh):
    torus = Mesh(
        mesh.devices.reshape(4, 2, 4, 2, mesh.shape["mz"]), ("mx_0", "mx_1", "my_0", "my_1", "mz")
    )
    in_specs = (
        P(None, MX, MY, "mz"),
        P(None, MX, MY, "mz"),
        P(MX, MY, "mz"),
        P(MX, MY, "mz"),
        P(MX, MY, "mz"),
        P(),
        P(MX, None),
        P(MX, None),
    )
    out_specs = (P(None, MX, MY, "mz"), P(MX, MY, "mz"), P(MX, None))
    return jax.shard_map(local, mesh=torus, in_specs=in_specs, out_specs=out_specs, check_vma=False)
```

profile of v0, /device:TPU:1, one launch (start us, length us, event | category | flops | bytes accessed | tf_op | source)
XLA Modules:
  0.0 1083.9 jit_solution(2123596516597603542)
XLA Ops:
  108.6 7.5 collective-permute-start.16
  124.8 7.8 all-reduce.108
  138.6 10.1 all-reduce.96
  153.2 6.6 all-reduce.120
  168.4 6.3 collective-permute-start.19
  201.8 6.8 all-reduce.107
  213.4 6.7 all-reduce.95
  243.3 6.3 collective-permute-start.25
  276.1 6.6 all-reduce.106
  287.6 8.2 all-reduce.94
  319.0 6.6 collective-permute-start.31
  335.2 6.5 collective-permute-start.34
  354.8 8.3 all-reduce.105
  367.2 7.5 all-reduce.93
  396.5 6.5 collective-permute-start.37
  427.2 6.8 all-reduce.104
  433.9 6.2 all-reduce.140
  440.2 7.2 all-reduce.92
  474.5 6.9 collective-permute-start.43
  486.8 6.3 collective-permute-start.46
  502.3 6.7 all-reduce.103
  515.3 7.2 all-reduce.91
  527.0 6.2 all-reduce.115
  538.5 6.2 collective-permute-start.49
  608.0 6.4 collective-permute-start.58
  622.3 6.7 all-reduce.102
  634.8 7.8 all-reduce.90
  647.2 7.1 all-reduce.114
  693.5 6.8 all-reduce.101
  705.8 7.2 all-reduce.89
  717.5 6.6 all-reduce.113
  754.1 7.2 collective-permute-start.70
  774.3 6.7 all-reduce.100
  781.0 6.4 all-reduce.136
  787.4 7.2 all-reduce.88
  818.8 6.4 collective-permute-start.73
  834.1 7.4 collective-permute-start.76
  855.7 7.2 all-reduce.99
  868.0 7.2 all-reduce.87
  896.8 6.5 collective-permute-start.79
  913.2 6.2 collective-permute-start.82
  933.6 7.8 all-reduce.98
  946.3 7.6 all-reduce.86
  981.3 7.1 collective-permute-start.85
  1011.0 6.7 all-reduce.97
  1023.5 7.2 all-reduce.85
  1059.1 6.6 all-to-all-start
  1066.6 8.0 collective-permute-start.90
  (709 shorter events, 698.1 us)
Async XLA Ops:
  1.6 46.0 %collective-permute-start.6 = (f32[3,2,32,128]{3,2,1,0:T(8,128)S(1)}, f32[3,2,32,128]{3,2,1,0:T(8,128)S(1)}, u32[]{:S(2)}, u32[]{:S(2)}) collective-permute-start(f32[3,2,32,128]{3,2,1,0:T(8,128)S(1)} %get-tuple-element.390), channel_id=1, source_target_pairs={{0,16},{16,32},{32,48},{48,64},{64,80},{80,96},{96,112},{1,17},{17... | collective-permute-start | bytes 294920 | tf_op jit(solution)/shard_map/ppermute | solution.py:61
  6.2 41.6 %collective-permute-start.7 = (f32[3,2,32,128]{3,2,1,0:T(8,128)S(1)}, f32[3,2,32,128]{3,2,1,0:T(8,128)S(1)}, u32[]{:S(2)}, u32[]{:S(2)}) collective-permute-start(f32[3,2,32,128]{3,2,1,0:T(8,128)S(1)} %get-tuple-element.389), channel_id=1, source_target_pairs={{16,0},{32,16},{48,32},{64,48},{80,64},{96,80},{112,96},{17,1},{33... | collective-permute-start | bytes 294920 | tf_op jit(solution)/shard_map/ppermute | solution.py:62
  10.0 22.7 %collective-permute-start.1 = (f32[2,1,32,128]{3,2,1,0:T(8,128)S(1)}, f32[2,1,32,128]{3,2,1,0:T(8,128)S(1)}, u32[]{:S(2)}, u32[]{:S(2)}) collective-permute-start(f32[2,1,32,128]{3,2,1,0:T(8,128)S(1)} %get-tuple-element.408), channel_id=1, source_target_pairs={{16,0},{32,16},{48,32},{64,48},{80,64},{96,80},{112,96},{17,1},{33... | collective-permute-start | bytes 98312 | tf_op jit(solution)/shard_map/ppermute | solution.py:62
  92.2 26.4 %collective-permute-start.15 = (f32[3,16,1,128]{3,1,2,0:T(8,128)}, f32[3,16,1,128]{3,1,2,0:T(8,128)}, u32[]{:S(2)}, u32[]{:S(2)}) collective-permute-start(f32[3,16,1,128]{3,1,2,0:T(8,128)} %bitcast.11), channel_id=1, source_target_pairs={{2,0},{4,2},{6,4},{8,6},{10,8},{12,10},{14,12},{3,1},{5,3},{7,5},{... | collective-permute-start | bytes 73736 | tf_op jit(solution)/shard_map/ppermute | solution.py:43
  93.5 26.7 %collective-permute-start.13 = (f32[3,1,32,128]{3,2,1,0:T(8,128)S(1)}, f32[3,1,32,128]{3,2,1,0:T(8,128)S(1)}, u32[]{:S(2)}, u32[]{:S(2)}) collective-permute-start(f32[3,1,32,128]{3,2,1,0:T(8,128)S(1)} %get-tuple-element.388), channel_id=1, source_target_pairs={{16,0},{32,16},{48,32},{64,48},{80,64},{96,80},{112,96},{17,1},{33... | collective-permute-start | bytes 147464 | tf_op jit(solution)/shard_map/ppermute | solution.py:43
  97.3 22.9 %collective-permute-start.12 = (f32[3,1,32,128]{3,2,1,0:T(8,128)S(1)}, f32[3,1,32,128]{3,2,1,0:T(8,128)S(1)}, u32[]{:S(2)}, u32[]{:S(2)}) collective-permute-start(f32[3,1,32,128]{3,2,1,0:T(8,128)S(1)} %get-tuple-element.387), channel_id=1, source_target_pairs={{0,16},{16,32},{32,48},{48,64},{64,80},{80,96},{96,112},{1,17},{17... | collective-permute-start | bytes 147464 | tf_op jit(solution)/shard_map/ppermute | solution.py:42
  167.1 27.2 %collective-permute-start.21 = (f32[3,16,1,128]{3,1,2,0:T(8,128)S(1)}, f32[3,16,1,128]{3,1,2,0:T(8,128)S(1)}, u32[]{:S(2)}, u32[]{:S(2)}) collective-permute-start(f32[3,16,1,128]{3,1,2,0:T(8,128)S(1)} %bitcast.174), channel_id=1, source_target_pairs={{2,0},{4,2},{6,4},{8,6},{10,8},{12,10},{14,12},{3,1},{5,3},{7,5},{... | collective-permute-start | bytes 73736 | tf_op jit(solution)/shard_map/ppermute | solution.py:43
  168.4 28.5 %collective-permute-start.19 = (f32[3,1,32,128]{3,2,1,0:T(8,128)S(1)}, f32[3,1,32,128]{3,2,1,0:T(8,128)S(1)}, u32[]{:S(2)}, u32[]{:S(2)}) collective-permute-start(f32[3,1,32,128]{3,2,1,0:T(8,128)S(1)} %get-tuple-element.382), channel_id=1, source_target_pairs={{16,0},{32,16},{48,32},{64,48},{80,64},{96,80},{112,96},{17,1},{33... | collective-permute-start | bytes 147464 | tf_op jit(solution)/shard_map/ppermute | solution.py:43
  174.7 22.2 %collective-permute-start.18 = (f32[3,1,32,128]{3,2,1,0:T(8,128)S(1)}, f32[3,1,32,128]{3,2,1,0:T(8,128)S(1)}, u32[]{:S(2)}, u32[]{:S(2)}) collective-permute-start(f32[3,1,32,128]{3,2,1,0:T(8,128)S(1)} %get-tuple-element.381), channel_id=1, source_target_pairs={{0,16},{16,32},{32,48},{48,64},{64,80},{80,96},{96,112},{1,17},{17... | collective-permute-start | bytes 147464 | tf_op jit(solution)/shard_map/ppermute | solution.py:42
  190.1 60.9 %collective-permute-start.105 = (f32[1,256]{1,0:T(1,128)}, f32[1,256]{1,0:T(1,128)S(1)}, u32[]{:S(2)}, u32[]{:S(2)}) collective-permute-start(f32[1,256]{1,0:T(1,128)} %get-tuple-element.456), channel_id=1, source_target_pairs={{16,0},{32,16},{48,32},{64,48},{80,64},{96,80},{112,96},{17,1},{33... | collective-permute-start | bytes 3080 | tf_op jit(solution)/shard_map/ppermute | solution.py:62
  194.3 59.7 %collective-permute-start.104 = (f32[1,256]{1,0:T(1,128)}, f32[1,256]{1,0:T(1,128)S(1)}, u32[]{:S(2)}, u32[]{:S(2)}) collective-permute-start(f32[1,256]{1,0:T(1,128)} %get-tuple-element.455), channel_id=1, source_target_pairs={{0,16},{16,32},{32,48},{48,64},{64,80},{80,96},{96,112},{1,17},{17... | collective-permute-start | bytes 3080 | tf_op jit(solution)/shard_map/ppermute | solution.py:61
  242.0 29.1 %collective-permute-start.27 = (f32[3,16,1,128]{3,1,2,0:T(8,128)}, f32[3,16,1,128]{3,1,2,0:T(8,128)S(1)}, u32[]{:S(2)}, u32[]{:S(2)}) collective-permute-start(f32[3,16,1,128]{3,1,2,0:T(8,128)} %bitcast.21), channel_id=1, source_target_pairs={{2,0},{4,2},{6,4},{8,6},{10,8},{12,10},{14,12},{3,1},{5,3},{7,5},{... | collective-permute-start | bytes 73736 | tf_op jit(solution)/shard_map/ppermute | solution.py:43
  243.3 27.9 %collective-permute-start.25 = (f32[3,1,32,128]{3,2,1,0:T(8,128)}, f32[3,1,32,128]{3,2,1,0:T(8,128)S(1)}, u32[]{:S(2)}, u32[]{:S(2)}) collective-permute-start(f32[3,1,32,128]{3,2,1,0:T(8,128)} %get-tuple-element.376), channel_id=1, source_target_pairs={{16,0},{32,16},{48,32},{64,48},{80,64},{96,80},{112,96},{17,1},{33... | collective-permute-start | bytes 147464 | tf_op jit(solution)/shard_map/ppermute | solution.py:43
  266.9 63.4 %collective-permute-start.98 = (f32[1,256]{1,0:T(1,128)S(1)}, f32[1,256]{1,0:T(1,128)S(1)}, u32[]{:S(2)}, u32[]{:S(2)}) collective-permute-start(f32[1,256]{1,0:T(1,128)S(1)} %copy-done.120), channel_id=1, source_target_pairs={{0,16},{16,32},{32,48},{48,64},{64,80},{80,96},{96,112},{1,17},{17... | collective-permute-start | bytes 3080 | tf_op jit(solution)/shard_map/ppermute | solution.py:61
  317.7 30.9 %collective-permute-start.33 = (f32[3,16,1,128]{3,1,2,0:T(8,128)}, f32[3,16,1,128]{3,1,2,0:T(8,128)}, u32[]{:S(2)}, u32[]{:S(2)}) collective-permute-start(f32[3,16,1,128]{3,1,2,0:T(8,128)} %bitcast.160), channel_id=1, source_target_pairs={{2,0},{4,2},{6,4},{8,6},{10,8},{12,10},{14,12},{3,1},{5,3},{7,5},{... | collective-permute-start | bytes 73736 | tf_op jit(solution)/shard_map/ppermute | solution.py:43
  319.0 31.2 %collective-permute-start.31 = (f32[3,1,32,128]{3,2,1,0:T(8,128)}, f32[3,1,32,128]{3,2,1,0:T(8,128)}, u32[]{:S(2)}, u32[]{:S(2)}) collective-permute-start(f32[3,1,32,128]{3,2,1,0:T(8,128)} %get-tuple-element.370), channel_id=1, source_target_pairs={{16,0},{32,16},{48,32},{64,48},{80,64},{96,80},{112,96},{17,1},{33... | collective-permute-start | bytes 147464 | tf_op jit(solution)/shard_map/ppermute | solution.py:43
  325.6 24.6 %collective-permute-start.30 = (f32[3,1,32,128]{3,2,1,0:T(8,128)}, f32[3,1,32,128]{3,2,1,0:T(8,128)}, u32[]{:S(2)}, u32[]{:S(2)}) collective-permute-start(f32[3,1,32,128]{3,2,1,0:T(8,128)} %get-tuple-element.369), channel_id=1, source_target_pairs={{0,16},{16,32},{32,48},{48,64},{64,80},{80,96},{96,112},{1,17},{17... | collective-permute-start | bytes 147464 | tf_op jit(solution)/shard_map/ppermute | solution.py:42
  343.6 62.8 %collective-permute-start.99 = (f32[1,256]{1,0:T(1,128)}, f32[1,256]{1,0:T(1,128)}, u32[]{:S(2)}, u32[]{:S(2)}) collective-permute-start(f32[1,256]{1,0:T(1,128)} %get-tuple-element.413), channel_id=1, source_target_pairs={{16,0},{32,16},{48,32},{64,48},{80,64},{96,80},{112,96},{17,1},{33... | collective-permute-start | bytes 3080 | tf_op jit(solution)/shard_map/ppermute | solution.py:62
  395.2 25.8 %collective-permute-start.39 = (f32[3,16,1,128]{3,1,2,0:T(8,128)}, f32[3,16,1,128]{3,1,2,0:T(8,128)}, u32[]{:S(2)}, u32[]{:S(2)}) collective-permute-start(f32[3,16,1,128]{3,1,2,0:T(8,128)} %bitcast.31), channel_id=1, source_target_pairs={{2,0},{4,2},{6,4},{8,6},{10,8},{12,10},{14,12},{3,1},{5,3},{7,5},{... | collective-permute-start | bytes 73736 | tf_op jit(solution)/shard_map/ppermute | solution.py:43
  396.5 26.1 %collective-permute-start.37 = (f32[3,1,32,128]{3,2,1,0:T(8,128)}, f32[3,1,32,128]{3,2,1,0:T(8,128)}, u32[]{:S(2)}, u32[]{:S(2)}) collective-permute-start(f32[3,1,32,128]{3,2,1,0:T(8,128)} %get-tuple-element.364), channel_id=1, source_target_pairs={{16,0},{32,16},{48,32},{64,48},{80,64},{96,80},{112,96},{17,1},{33... | collective-permute-start | bytes 147464 | tf_op jit(solution)/shard_map/ppermute | solution.py:43
  468.6 28.3 %collective-permute-start.45 = (f32[3,16,1,128]{3,1,2,0:T(8,128)}, f32[3,16,1,128]{3,1,2,0:T(8,128)}, u32[]{:S(2)}, u32[]{:S(2)}) collective-permute-start(f32[3,16,1,128]{3,1,2,0:T(8,128)} %bitcast.169), channel_id=1, source_target_pairs={{2,0},{4,2},{6,4},{8,6},{10,8},{12,10},{14,12},{3,1},{5,3},{7,5},{... | collective-permute-start | bytes 73736 | tf_op jit(solution)/shard_map/ppermute | solution.py:43
  469.9 27.8 %collective-permute-start.44 = (f32[3,16,1,128]{3,1,2,0:T(8,128)}, f32[3,16,1,128]{3,1,2,0:T(8,128)}, u32[]{:S(2)}, u32[]{:S(2)}) collective-permute-start(f32[3,16,1,128]{3,1,2,0:T(8,128)} %bitcast.161), channel_id=1, source_target_pairs={{0,2},{2,4},{4,6},{6,8},{8,10},{10,12},{12,14},{1,3},{3,5},{5,7},{... | collective-permute-start | bytes 73736 | tf_op jit(solution)/shard_map/ppermute | solution.py:42
  474.5 24.0 %collective-permute-start.43 = (f32[3,1,32,128]{3,2,1,0:T(8,128)}, f32[3,1,32,128]{3,2,1,0:T(8,128)}, u32[]{:S(2)}, u32[]{:S(2)}) collective-permute-start(f32[3,1,32,128]{3,2,1,0:T(8,128)} %get-tuple-element.356), channel_id=1, source_target_pairs={{16,0},{32,16},{48,32},{64,48},{80,64},{96,80},{112,96},{17,1},{33... | collective-permute-start | bytes 147464 | tf_op jit(solution)/shard_map/ppermute | solution.py:43
  559.8 43.2 %collective-permute-start.101 = (f32[1,256]{1,0:T(1,128)}, f32[1,256]{1,0:T(1,128)}, u32[]{:S(2)}, u32[]{:S(2)}) collective-permute-start(f32[1,256]{1,0:T(1,128)} %get-tuple-element.411), channel_id=1, source_target_pairs={{16,0},{32,16},{48,32},{64,48},{80,64},{96,80},{112,96},{17,1},{33... | collective-permute-start | bytes 3080 | tf_op jit(solution)/shard_map/ppermute | solution.py:62
  594.1 23.4 %collective-permute-start.57 = (f32[3,16,1,128]{3,1,2,0:T(8,128)}, f32[3,16,1,128]{3,1,2,0:T(8,128)S(1)}, u32[]{:S(2)}, u32[]{:S(2)}) collective-permute-start(f32[3,16,1,128]{3,1,2,0:T(8,128)} %bitcast.47), channel_id=1, source_target_pairs={{2,0},{4,2},{6,4},{8,6},{10,8},{12,10},{14,12},{3,1},{5,3},{7,5},{... | collective-permute-start | bytes 73736 | tf_op jit(solution)/shard_map/ppermute | solution.py:43
  595.4 22.2 %collective-permute-start.55 = (f32[3,1,32,128]{3,2,1,0:T(8,128)S(1)}, f32[3,1,32,128]{3,2,1,0:T(8,128)S(1)}, u32[]{:S(2)}, u32[]{:S(2)}) collective-permute-start(f32[3,1,32,128]{3,2,1,0:T(8,128)S(1)} %get-tuple-element.350), channel_id=1, source_target_pairs={{16,0},{32,16},{48,32},{64,48},{80,64},{96,80},{112,96},{17,1},{33... | collective-permute-start | bytes 147464 | tf_op jit(solution)/shard_map/ppermute | solution.py:43
  662.4 24.7 %collective-permute-start.63 = (f32[3,16,1,128]{3,1,2,0:T(8,128)}, f32[3,16,1,128]{3,1,2,0:T(8,128)}, u32[]{:S(2)}, u32[]{:S(2)}) collective-permute-start(f32[3,16,1,128]{3,1,2,0:T(8,128)} %bitcast.52), channel_id=1, source_target_pairs={{2,0},{4,2},{6,4},{8,6},{10,8},{12,10},{14,12},{3,1},{5,3},{7,5},{... | collective-permute-start | bytes 73736 | tf_op jit(solution)/shard_map/ppermute | solution.py:43
  663.7 25.0 %collective-permute-start.61 = (f32[3,1,32,128]{3,2,1,0:T(8,128)}, f32[3,1,32,128]{3,2,1,0:T(8,128)S(1)}, u32[]{:S(2)}, u32[]{:S(2)}) collective-permute-start(f32[3,1,32,128]{3,2,1,0:T(8,128)} %get-tuple-element.344), channel_id=1, source_target_pairs={{16,0},{32,16},{48,32},{64,48},{80,64},{96,80},{112,96},{17,1},{33... | collective-permute-start | bytes 147464 | tf_op jit(solution)/shard_map/ppermute | solution.py:43
  736.3 31.7 %collective-permute-start.69 = (f32[3,16,1,128]{3,1,2,0:T(8,128)}, f32[3,16,1,128]{3,1,2,0:T(8,128)}, u32[]{:S(2)}, u32[]{:S(2)}) collective-permute-start(f32[3,16,1,128]{3,1,2,0:T(8,128)} %bitcast.171), channel_id=1, source_target_pairs={{2,0},{4,2},{6,4},{8,6},{10,8},{12,10},{14,12},{3,1},{5,3},{7,5},{... | collective-permute-start | bytes 73736 | tf_op jit(solution)/shard_map/ppermute | solution.py:43
  737.6 32.0 %collective-permute-start.67 = (f32[3,1,32,128]{3,2,1,0:T(8,128)}, f32[3,1,32,128]{3,2,1,0:T(8,128)}, u32[]{:S(2)}, u32[]{:S(2)}) collective-permute-start(f32[3,1,32,128]{3,2,1,0:T(8,128)} %get-tuple-element.338), channel_id=1, source_target_pairs={{16,0},{32,16},{48,32},{64,48},{80,64},{96,80},{112,96},{17,1},{33... | collective-permute-start | bytes 147464 | tf_op jit(solution)/shard_map/ppermute | solution.py:43
  743.6 25.9 %collective-permute-start.66 = (f32[3,1,32,128]{3,2,1,0:T(8,128)}, f32[3,1,32,128]{3,2,1,0:T(8,128)}, u32[]{:S(2)}, u32[]{:S(2)}) collective-permute-start(f32[3,1,32,128]{3,2,1,0:T(8,128)} %get-tuple-element.337), channel_id=1, source_target_pairs={{0,16},{16,32},{32,48},{48,64},{64,80},{80,96},{96,112},{1,17},{17... | collective-permute-start | bytes 147464 | tf_op jit(solution)/shard_map/ppermute | solution.py:42
  747.1 21.6 %collective-permute-start.68 = (f32[3,16,1,128]{3,1,2,0:T(8,128)}, f32[3,16,1,128]{3,1,2,0:T(8,128)}, u32[]{:S(2)}, u32[]{:S(2)}) collective-permute-start(f32[3,16,1,128]{3,1,2,0:T(8,128)} %bitcast.162), channel_id=1, source_target_pairs={{0,2},{2,4},{4,6},{6,8},{8,10},{10,12},{12,14},{1,3},{3,5},{5,7},{... | collective-permute-start | bytes 73736 | tf_op jit(solution)/shard_map/ppermute | solution.py:42
  817.5 32.0 %collective-permute-start.75 = (f32[3,16,1,128]{3,1,2,0:T(8,128)}, f32[3,16,1,128]{3,1,2,0:T(8,128)}, u32[]{:S(2)}, u32[]{:S(2)}) collective-permute-start(f32[3,16,1,128]{3,1,2,0:T(8,128)} %bitcast.172), channel_id=1, source_target_pairs={{2,0},{4,2},{6,4},{8,6},{10,8},{12,10},{14,12},{3,1},{5,3},{7,5},{... | collective-permute-start | bytes 73736 | tf_op jit(solution)/shard_map/ppermute | solution.py:43
  818.8 32.3 %collective-permute-start.73 = (f32[3,1,32,128]{3,2,1,0:T(8,128)}, f32[3,1,32,128]{3,2,1,0:T(8,128)}, u32[]{:S(2)}, u32[]{:S(2)}) collective-permute-start(f32[3,1,32,128]{3,2,1,0:T(8,128)} %get-tuple-element.332), channel_id=1, source_target_pairs={{16,0},{32,16},{48,32},{64,48},{80,64},{96,80},{112,96},{17,1},{33... | collective-permute-start | bytes 147464 | tf_op jit(solution)/shard_map/ppermute | solution.py:43
  825.2 25.9 %collective-permute-start.72 = (f32[3,1,32,128]{3,2,1,0:T(8,128)}, f32[3,1,32,128]{3,2,1,0:T(8,128)}, u32[]{:S(2)}, u32[]{:S(2)}) collective-permute-start(f32[3,1,32,128]{3,2,1,0:T(8,128)} %get-tuple-element.331), channel_id=1, source_target_pairs={{0,16},{16,32},{32,48},{48,64},{64,80},{80,96},{96,112},{1,17},{17... | collective-permute-start | bytes 147464 | tf_op jit(solution)/shard_map/ppermute | solution.py:42
  827.1 23.1 %collective-permute-start.74 = (f32[3,16,1,128]{3,1,2,0:T(8,128)}, f32[3,16,1,128]{3,1,2,0:T(8,128)}, u32[]{:S(2)}, u32[]{:S(2)}) collective-permute-start(f32[3,16,1,128]{3,1,2,0:T(8,128)} %bitcast.165), channel_id=1, source_target_pairs={{0,2},{2,4},{4,6},{6,8},{8,10},{10,12},{12,14},{1,3},{3,5},{5,7},{... | collective-permute-start | bytes 73736 | tf_op jit(solution)/shard_map/ppermute | solution.py:42
  844.9 63.4 %collective-permute-start.102 = (f32[1,256]{1,0:T(1,128)S(1)}, f32[1,256]{1,0:T(1,128)S(1)}, u32[]{:S(2)}, u32[]{:S(2)}) collective-permute-start(f32[1,256]{1,0:T(1,128)S(1)} %get-tuple-element.410), channel_id=1, source_target_pairs={{0,16},{16,32},{32,48},{48,64},{64,80},{80,96},{96,112},{1,17},{17... | collective-permute-start | bytes 3080 | tf_op jit(solution)/shard_map/ppermute | solution.py:61
  895.5 31.8 %collective-permute-start.81 = (f32[3,16,1,128]{3,1,2,0:T(8,128)}, f32[3,16,1,128]{3,1,2,0:T(8,128)}, u32[]{:S(2)}, u32[]{:S(2)}) collective-permute-start(f32[3,16,1,128]{3,1,2,0:T(8,128)} %bitcast.163), channel_id=1, source_target_pairs={{2,0},{4,2},{6,4},{8,6},{10,8},{12,10},{14,12},{3,1},{5,3},{7,5},{... | collective-permute-start | bytes 73736 | tf_op jit(solution)/shard_map/ppermute | solution.py:43
  896.8 32.1 %collective-permute-start.79 = (f32[3,1,32,128]{3,2,1,0:T(8,128)}, f32[3,1,32,128]{3,2,1,0:T(8,128)}, u32[]{:S(2)}, u32[]{:S(2)}) collective-permute-start(f32[3,1,32,128]{3,2,1,0:T(8,128)} %get-tuple-element.326), channel_id=1, source_target_pairs={{16,0},{32,16},{48,32},{64,48},{80,64},{96,80},{112,96},{17,1},{33... | collective-permute-start | bytes 147464 | tf_op jit(solution)/shard_map/ppermute | solution.py:43
  903.3 25.6 %collective-permute-start.78 = (f32[3,1,32,128]{3,2,1,0:T(8,128)}, f32[3,1,32,128]{3,2,1,0:T(8,128)}, u32[]{:S(2)}, u32[]{:S(2)}) collective-permute-start(f32[3,1,32,128]{3,2,1,0:T(8,128)} %get-tuple-element.325), channel_id=1, source_target_pairs={{0,16},{16,32},{32,48},{48,64},{64,80},{80,96},{96,112},{1,17},{17... | collective-permute-start | bytes 147464 | tf_op jit(solution)/shard_map/ppermute | solution.py:42
  923.3 67.2 %collective-permute-start.103 = (f32[1,256]{1,0:T(1,128)S(1)}, f32[1,256]{1,0:T(1,128)S(1)}, u32[]{:S(2)}, u32[]{:S(2)}) collective-permute-start(f32[1,256]{1,0:T(1,128)S(1)} %get-tuple-element.409), channel_id=1, source_target_pairs={{16,0},{32,16},{48,32},{64,48},{80,64},{96,80},{112,96},{17,1},{33... | collective-permute-start | bytes 3080 | tf_op jit(solution)/shard_map/ppermute | solution.py:62
  975.4 28.1 %collective-permute-start.87 = (f32[3,16,1,128]{3,1,2,0:T(8,128)}, f32[3,16,1,128]{3,1,2,0:T(8,128)}, u32[]{:S(2)}, u32[]{:S(2)}) collective-permute-start(f32[3,16,1,128]{3,1,2,0:T(8,128)} %bitcast.167), channel_id=1, source_target_pairs={{2,0},{4,2},{6,4},{8,6},{10,8},{12,10},{14,12},{3,1},{5,3},{7,5},{... | collective-permute-start | bytes 73736 | tf_op jit(solution)/shard_map/ppermute | solution.py:43
  976.7 27.6 %collective-permute-start.86 = (f32[3,16,1,128]{3,1,2,0:T(8,128)}, f32[3,16,1,128]{3,1,2,0:T(8,128)}, u32[]{:S(2)}, u32[]{:S(2)}) collective-permute-start(f32[3,16,1,128]{3,1,2,0:T(8,128)} %bitcast.159), channel_id=1, source_target_pairs={{0,2},{2,4},{4,6},{6,8},{8,10},{10,12},{12,14},{1,3},{3,5},{5,7},{... | collective-permute-start | bytes 73736 | tf_op jit(solution)/shard_map/ppermute | solution.py:42
  981.3 23.8 %collective-permute-start.85 = (f32[3,1,32,128]{3,2,1,0:T(8,128)}, f32[3,1,32,128]{3,2,1,0:T(8,128)}, u32[]{:S(2)}, u32[]{:S(2)}) collective-permute-start(f32[3,1,32,128]{3,2,1,0:T(8,128)} %get-tuple-element.318), channel_id=1, source_target_pairs={{16,0},{32,16},{48,32},{64,48},{80,64},{96,80},{112,96},{17,1},{33... | collective-permute-start | bytes 147464 | tf_op jit(solution)/shard_map/ppermute | solution.py:43
  1047.4 27.2 %collective-permute-start.95 = (f32[3,16,32,1]{2,1,3,0:T(8,128)S(1)}, f32[3,16,32,1]{2,1,3,0:T(8,128)S(1)}, u32[]{:S(2)}, u32[]{:S(2)}) collective-permute-start(f32[3,16,32,1]{2,1,3,0:T(8,128)S(1)} %copy.1548), channel_id=1, source_target_pairs={{0,1},{2,3},{4,5},{6,7},{8,9},{10,11},{12,13},{14,15},{16,17},{18,... | collective-permute-start | bytes 18440 | tf_op jit(solution)/shard_map/ppermute | solution.py:42
  1051.4 27.4 %collective-permute-start.92 = (f32[3,16,1,128]{3,1,2,0:T(8,128)S(1)}, f32[3,16,1,128]{3,1,2,0:T(8,128)S(1)}, u32[]{:S(2)}, u32[]{:S(2)}) collective-permute-start(f32[3,16,1,128]{3,1,2,0:T(8,128)S(1)} %bitcast.173), channel_id=1, source_target_pairs={{2,0},{4,2},{6,4},{8,6},{10,8},{12,10},{14,12},{3,1},{5,3},{7,5},{... | collective-permute-start | bytes 73736 | tf_op jit(solution)/shard_map/ppermute | solution.py:43
  1052.7 26.2 %collective-permute-start.93 = (f32[3,16,1,128]{3,1,2,0:T(8,128)S(1)}, f32[3,16,1,128]{3,1,2,0:T(8,128)S(1)}, u32[]{:S(2)}, u32[]{:S(2)}) collective-permute-start(f32[3,16,1,128]{3,1,2,0:T(8,128)S(1)} %bitcast.168), channel_id=1, source_target_pairs={{0,2},{2,4},{4,6},{6,8},{8,10},{10,12},{12,14},{1,3},{3,5},{5,7},{... | collective-permute-start | bytes 73736 | tf_op jit(solution)/shard_map/ppermute | solution.py:42
  1057.1 21.4 %collective-permute-start.94 = (f32[3,16,32,1]{2,1,3,0:T(8,128)S(1)}, f32[3,16,32,1]{2,1,3,0:T(8,128)S(1)}, u32[]{:S(2)}, u32[]{:S(2)}) collective-permute-start(f32[3,16,32,1]{2,1,3,0:T(8,128)S(1)} %copy.1546), channel_id=1, source_target_pairs={{1,0},{3,2},{5,4},{7,6},{9,8},{11,10},{13,12},{15,14},{17,16},{19,... | collective-permute-start | bytes 18440 | tf_op jit(solution)/shard_map/ppermute | solution.py:43
  (180 other events, 3666.2 us)
where the time goes:
time: 1100 us; the launch traced here: 1080 us
  starting transfers between devices  384 us (35%)
  blocking collectives  370 us (34%)
  local copies, waits for them, and re-layouts  153 us (14%)
  other arithmetic  125 us (11%)
  between operations  49.7 us (5%)
    psum x60, blocking collectives, by_axis(): return functools.reduce(lax.psum, axes, array)  370 us
    ppermute x39, starting transfers between devices, with_halo(): lax.ppermute(last, axis, up)  180 us
    ppermute x39, starting transfers between devices, with_halo(): lax.ppermute(initial, axis, [(b, a) for a, b in up])  112 us
    reduce_sum x12, other arithmetic, paired_products(): jnp.sum(residual * applied)  56.6 us
    ppermute x14, starting transfers between devices, extended(): before = lax.ppermute(last, axis, up)  55.6 us
    slice x51, local copies, waits for them, and re-layouts, with_halo(): last = lax.slice_in_dim(array, length - width, length, axis=dim)  54 us
    ppermute x14, starting transfers between devices, extended(): after = lax.ppermute(initial, axis, down)  30.5 us
  transfers between devices with their start and end apart: 107, of which 2 were waited for; matrix products, arithmetic and copies ran while one was open for 17% of the time, Pallas kernels for 0%

commit v1 on v0

v1 whole, which is shorter than its diff:
```python
import functools
import math

import jax
import jax.numpy as jnp
from jax import lax
from jax.experimental import pallas as pl
from jax.experimental.pallas import tpu as pltpu
from jax.sharding import PartitionSpec as P

KMAX = 6
SWEEPS = 4
NXL, NYL, NZL = 16, 32, 128
PADY = 8
LO, HI = PADY, PADY + NYL
BUFY = PADY + NYL + PADY
RIM = 8

drag_coef = 0.05
cohesion_base = 1.0
weakening = 0.6
critical_strain = 1.0
sin_friction = 0.5
cos_friction = 0.8660254
pressure_gradient = 2.0
rate_floor = 0.1
strain_step = 0.5
uplift_gain = 8.0
surface_step = 0.2
erodibility = 0.5
neighbour_steps = ((-1, -1), (-1, 0), (-1, 1), (0, -1), (0, 1), (1, -1), (1, 0), (1, 1))

MESH = pl.DeviceIdType.MESH
U_SET, E_SET = 2, 3
f32 = jnp.float32


def step_kernel(
    counts, px, py, pz,
    force, vel, visc, strain, flags, heights, receivers,
    vout, sout, tout,
    ubuf, ebuf, wbuf, ys, yr, zs, zr, strength, coef, r, p, s, z, q, sums1, sums2, surf, base, tiles,
    face_send, face_recv, one_send, one_recv, two_send, two_recv, surf_send, surf_recv, tile_send, tile_recv,
):
    mx, my, mz = lax.axis_index("mx"), lax.axis_index("my"), lax.axis_index("mz")
    group = py * pz
    place = my * pz + mz
    edge = (NZL - 1) * (1 - mz)

    def at_group(k):
        other = lax.rem(place + k, group)
        return {"my": other // pz, "mz": lax.rem(other, pz)}

    def at_row(k):
        return {"mx": lax.rem(mx + k, px)}

    def lanes(rows):
        return lax.broadcasted_iota(jnp.int32, (rows, NZL), 1)

    def blank(buf, parts):
        zero = jnp.zeros((NYL, NZL), f32)
        row = jnp.zeros((1, NZL), f32)

        def clear(i, _):
            for c in range(parts):
                buf[c, i, LO - 1 : LO, :] = row
                buf[c, i, HI : HI + 1, :] = row
            return 0

        lax.fori_loop(0, NXL + 2, clear, 0)
        for c in range(parts):
            buf[c, 0, LO:HI, :] = zero
            buf[c, NXL + 1, LO:HI, :] = zero

    blank(ubuf, 3)
    blank(ebuf, 1)
    blank(wbuf.at[0], 3)
    blank(wbuf.at[1], 3)
    for kind in range(4):
        for side in range(2):
            for c in range(3):
                yr[kind, side, c] = jnp.zeros((NXL, NZL), f32)
    rows, cols = surf.shape[1:]
    surf[0, 0:RIM, :] = jnp.full((RIM, cols), -1.0, f32)
    surf[0, RIM + NXL :, :] = jnp.full((RIM, cols), -1.0, f32)
    surf[1, 0:RIM, :] = jnp.zeros((RIM, cols), f32)
    surf[1, RIM + NXL :, :] = jnp.zeros((RIM, cols), f32)
    surf[0, RIM : RIM + NXL, :] = receivers[...].astype(f32)
    surf[1, RIM : RIM + NXL, :] = heights[...]

    barrier = pltpu.get_barrier_semaphore()
    for k in range(1, px):
        pl.semaphore_signal(barrier, inc=1, device_id=at_row(k), device_id_type=MESH)
    for k in range(1, group):
        pl.semaphore_signal(barrier, inc=1, device_id=at_group(k), device_id_type=MESH)

    def face_copy(kind, d, src, dst, device):
        return pltpu.make_async_remote_copy(
            src_ref=src, dst_ref=dst, send_sem=face_send.at[kind, d], recv_sem=face_recv.at[kind, d],
            device_id=device, device_id_type=MESH,
        )

    def face_copies(buf, kind, n):
        comps = slice(0, n)
        return (
            (mx < px - 1, mx > 0, 0, buf.at[comps, NXL, LO:HI, :], buf.at[comps, 0, LO:HI, :], {"mx": mx + 1}),
            (mx > 0, mx < px - 1, 1, buf.at[comps, 1, LO:HI, :], buf.at[comps, NXL + 1, LO:HI, :], {"mx": mx - 1}),
            (my < py - 1, my > 0, 2, ys.at[kind, 1, comps], yr.at[kind, 0, comps], {"my": my + 1}),
            (my > 0, my < py - 1, 3, ys.at[kind, 0, comps], yr.at[kind, 1, comps], {"my": my - 1}),
        )

    def depth_copy(kind):
        return face_copy(kind, 4, zs.at[kind], zr.at[kind], {"mz": 1 - mz})

    def start_faces(buf, kind, n):
        depth_copy(kind).start()
        for sends, _, d, src, dst, device in face_copies(buf, kind, n):
            @pl.when(sends)
            def _():
                face_copy(kind, d, src, dst, device).start()

    def finish_faces(buf, kind, n):
        for sends, receives, d, src, dst, device in face_copies(buf, kind, n):
            @pl.when(sends)
            def _():
                face_copy(kind, d, src, dst, device).wait_send()

            @pl.when(receives)
            def _():
                face_copy(kind, d, src, dst, device).wait_recv()
        depth_copy(kind).wait()
        for c in range(n):
            low, high = yr[kind, 0, c], yr[kind, 1, c]
            for x in range(NXL):
                buf[c, x + 1, LO - 1 : LO, :] = low[x : x + 1]
                buf[c, x + 1, HI : HI + 1, :] = high[x : x + 1]

    half = NYL // 2
    lane_half = lanes(half)
    lane_full = lanes(NYL)

    def pack(kind, c, x, plane, held):
        ys[kind, 0, c, pl.ds(x, 1), :] = plane[0:1]
        ys[kind, 1, c, pl.ds(x, 1), :] = plane[NYL - 1 :]
        for part in range(2):
            spot = c * NXL + x + 48 * part
            turned = pltpu.roll(plane[part * half : (part + 1) * half], lax.rem(spot - edge + NZL, NZL), 1)
            held = jnp.where(lane_half == spot, turned, held)
        return held

    no_pack = jnp.zeros((half, NZL), f32)

    def depth_pair(v, arrived, c, x):
        parts = []
        for part in range(2):
            spot = c * NXL + x + 48 * part
            parts.append(pltpu.roll(arrived, lax.rem(edge - spot + NZL, NZL), 1))
        rim = jnp.where(lane_full == edge, jnp.concatenate(parts, axis=0), 0.0)
        below = jnp.where(lane_full == 0, rim, pltpu.roll(v, 1, 1))
        above = jnp.where(lane_full == NZL - 1, rim, pltpu.roll(v, NZL - 1, 1))
        return below, above

    def around(buf, arrived, c, x):
        v = buf[c, x + 1, LO:HI, :]
        below, above = depth_pair(v, arrived, c, x)
        return v, (
            (buf[c, x, LO:HI, :], buf[c, x + 2, LO:HI, :]),
            (buf[c, x + 1, LO - 1 : HI - 1, :], buf[c, x + 1, LO + 1 : HI + 1, :]),
            (below, above),
        )

    def applied(buf, arrived, c, x):
        v, pairs = around(buf, arrived, c, x)
        total = coef[6, x] * v
        for d in range(3):
            total = total - coef[2 * d, x] * pairs[d][0] - coef[2 * d + 1, x] * pairs[d][1]
        return v, total

    def rate_at(x, arrived):
        g = []
        for c in range(3):
            _, pairs = around(ubuf, arrived, c, x)
            g.append([0.5 * (pair[1] - pair[0]) for pair in pairs])
        total = g[0][0] * g[0][0] + g[1][1] * g[1][1] + g[2][2] * g[2][2]
        for a, b in ((0, 1), (0, 2), (1, 2)):
            shear = g[a][b] + g[b][a]
            total = total + 0.5 * (shear * shear)
        return jnp.sqrt(0.5 * total)

    def planes(body, carry, unroll=2):
        return lax.fori_loop(0, NXL, body, carry, unroll=unroll)

    def one_copy(slot, k):
        mine = sums1.at[slot, mx]
        return pltpu.make_async_remote_copy(
            src_ref=mine, dst_ref=mine, send_sem=one_send.at[slot, k], recv_sem=one_recv.at[slot, k],
            device_id=at_row(k), device_id_type=MESH,
        )

    def two_copy(slot, k):
        mine = sums2.at[slot, place]
        return pltpu.make_async_remote_copy(
            src_ref=mine, dst_ref=mine, send_sem=two_send.at[slot, k], recv_sem=two_recv.at[slot, k],
            device_id=at_group(k), device_id_type=MESH,
        )

    def start_sums(slot, gg, dd):
        sums1[slot, mx] = jnp.concatenate(
            [jnp.sum(gg, axis=0, keepdims=True), jnp.sum(dd, axis=0, keepdims=True)], axis=0
        )
        for k in range(1, px):
            one_copy(slot, k).start()

    def middle_sums(slot):
        for k in range(1, px):
            one_copy(slot, k).wait()
        sums2[slot, place] = jnp.sum(sums1[slot], axis=0)
        for k in range(1, group):
            two_copy(slot, k).start()

    def finish_sums(slot):
        for k in range(1, group):
            two_copy(slot, k).wait()
        both = jnp.sum(jnp.sum(sums2[slot], axis=0), axis=1, keepdims=True)
        both = jnp.broadcast_to(both, (2, NZL))
        return both[0:1], both[1:2]

    def load(x, held):
        for c in range(3):
            plane = vel[c, x]
            ubuf[c, x + 1, LO:HI, :] = plane
            held = pack(U_SET, c, x, plane, held)
        return held

    zs[U_SET] = planes(load, no_pack)
    pl.semaphore_wait(barrier, px - 1 + group - 1)
    start_faces(ubuf, U_SET, 3)

    def surf_copy(d):
        if d == 0:
            src, dst, device = surf.at[:, NXL : NXL + RIM], surf.at[:, 0:RIM], {"mx": mx + 1}
        else:
            src, dst, device = surf.at[:, RIM : 2 * RIM], surf.at[:, RIM + NXL : RIM + NXL + RIM], {"mx": mx - 1}
        return pltpu.make_async_remote_copy(
            src_ref=src, dst_ref=dst, send_sem=surf_send.at[d], recv_sem=surf_recv.at[d],
            device_id=device, device_id_type=MESH,
        )

    for d, sends in ((0, mx < px - 1), (1, mx > 0)):
        @pl.when(sends)
        def _():
            surf_copy(d).start()

    depth_at = mz * NZL + lane_full
    pressure = pressure_gradient * (pz * NZL - 0.5 - depth_at.astype(f32)) / (pz * NZL)

    def strengthen(x, _):
        weak = flags[x].astype(f32) * jnp.minimum(strain[x] / critical_strain, 1.0)
        strength[x] = cohesion_base * (1.0 - weakening * weak) * cos_friction + pressure * sin_friction
        for c in range(3):
            zero = jnp.zeros((NYL, NZL), f32)
            p[c, x] = zero
            s[c, x] = zero
            z[c, x] = zero
        return 0

    planes(strengthen, 0)

    for d, sends, receives in ((0, mx < px - 1, mx > 0), (1, mx > 0, mx < px - 1)):
        @pl.when(sends)
        def _():
            surf_copy(d).wait_send()

        @pl.when(receives)
        def _():
            surf_copy(d).wait_recv()

    code = surf[0]
    col = lax.broadcasted_iota(jnp.int32, (rows, cols), 1)

    def turned(block, row_step, col_step):
        if col_step:
            block = pltpu.roll(block, col_step % cols, 1)
        if row_step:
            block = pltpu.roll(block, row_step % rows, 0)
        return block

    drained = jnp.ones((rows, cols), f32)
    for _ in range(SWEEPS):
        total = jnp.ones((rows, cols), f32)
        for direction, (row_step, col_step) in enumerate(neighbour_steps):
            chosen = code == float(direction)
            if col_step:
                chosen = chosen & (col != (cols - 1 if col_step > 0 else 0))
            total = total + turned(jnp.where(chosen, drained, 0.0), row_step, col_step)
        drained = total
    height = surf[1]
    below = jnp.zeros((rows, cols), f32)
    spacing = jnp.ones((rows, cols), f32)
    for direction, (row_step, col_step) in enumerate(neighbour_steps):
        chosen = code == float(direction)
        seen = chosen
        if col_step:
            seen = seen & (col != (cols - 1 if col_step > 0 else 0))
        below = below + jnp.where(seen, turned(height, -row_step, -col_step), 0.0)
        if row_step and col_step:
            spacing = jnp.where(chosen, math.sqrt(2.0), spacing)
    slope = jnp.maximum(height - below, 0.0) / spacing
    ground = height - (surface_step * erodibility) * jnp.sqrt(drained) * slope
    base[...] = ground[RIM : RIM + NXL]

    for picard, count in enumerate(counts):
        if picard:
            def resend(x, held):
                for c in range(3):
                    held = pack(U_SET, c, x, ubuf[c, x + 1, LO:HI, :], held)
                return held

            zs[U_SET] = planes(resend, no_pack)
            start_faces(ubuf, U_SET, 3)
        finish_faces(ubuf, U_SET, 3)
        u_rim = zr[U_SET]

        def soften(x, held):
            rate = rate_at(x, u_rim)
            eta = jnp.minimum(visc[x], strength[x] / (2.0 * jnp.maximum(rate, rate_floor)))
            ebuf[0, x + 1, LO:HI, :] = eta
            return pack(E_SET, 0, x, eta, held)

        zs[E_SET] = planes(soften, no_pack)
        start_faces(ebuf, E_SET, 1)
        finish_faces(ebuf, E_SET, 1)
        e_rim = zr[E_SET]

        def begin(x, held):
            eta, pairs = around(ebuf, e_rim, 0, x)
            total = jnp.full((NYL, NZL), drag_coef, f32)
            for d in range(3):
                for side in range(2):
                    face = 0.5 * (eta + pairs[d][side])
                    coef[2 * d + side, x] = face
                    total = total + face
            coef[6, x] = total
            for c in range(3):
                _, au = applied(ubuf, u_rim, c, x)
                plane = force[c, x] - au
                r[c, x] = plane
                wbuf[0, c, x + 1, LO:HI, :] = plane
                held = pack(0, c, x, plane, held)
            return held

        zs[0] = planes(begin, no_pack, 1)
        start_faces(wbuf.at[0], 0, 3)
        finish_faces(wbuf.at[0], 0, 3)
        r_rim = zr[0]
        nothing = jnp.zeros((NYL, NZL), f32)

        def first(x, carry):
            held, gg, dd = carry
            for c in range(3):
                v, w = applied(wbuf.at[0], r_rim, c, x)
                wbuf[1, c, x + 1, LO:HI, :] = w
                gg = gg + v * v
                dd = dd + v * w
                held = pack(1, c, x, w, held)
            return held, gg, dd

        held, gg, dd = planes(first, (no_pack, nothing, nothing))
        zs[1] = held
        start_sums(0, gg, dd)
        start_faces(wbuf.at[1], 1, 3)

        def scalars(i, gamma, delta, gamma_old, alpha_old):
            beta = jnp.where(i == 0, 0.0, gamma / gamma_old)
            alpha = gamma / (delta - beta * gamma / alpha_old)
            return alpha, beta

        def iterate(i, carry):
            gamma_old, alpha_old = carry
            now, later = lax.rem(i + 1, 2), lax.rem(i, 2)
            w_now, w_later = wbuf.at[now], wbuf.at[later]
            slot = lax.rem(i, 2)
            middle_sums(slot)
            finish_faces(w_now, now, 3)
            rim = zr[now]

            def again(x, _):
                for c in range(3):
                    q[c, x] = applied(w_now, rim, c, x)[1]
                return 0

            planes(again, 0)
            gamma, delta = finish_sums(slot)
            alpha, beta = scalars(i, gamma, delta, gamma_old, alpha_old)

            def update(x, carry):
                held, gg, dd = carry
                for c in range(3):
                    w = w_now[c, x + 1, LO:HI, :]
                    z_new = q[c, x] + beta * z[c, x]
                    s_new = w + beta * s[c, x]
                    r_old = r[c, x]
                    p_new = r_old + beta * p[c, x]
                    r_new = r_old - alpha * s_new
                    w_new = w - alpha * z_new
                    z[c, x] = z_new
                    s[c, x] = s_new
                    p[c, x] = p_new
                    r[c, x] = r_new
                    w_later[c, x + 1, LO:HI, :] = w_new
                    ubuf[c, x + 1, LO:HI, :] = ubuf[c, x + 1, LO:HI, :] + alpha * p_new
                    gg = gg + r_new * r_new
                    dd = dd + r_new * w_new
                    held = pack(later, c, x, w_new, held)
                return held, gg, dd

            held, gg, dd = planes(update, (no_pack, nothing, nothing))
            zs[later] = held
            start_sums(later_slot(i), gg, dd)

            @pl.when(i < count - 2)
            def _():
                start_faces(w_later, later, 3)

            return gamma, alpha

        def later_slot(i):
            return lax.rem(i + 1, 2)

        ones = jnp.ones((1, NZL), f32)
        gamma_old, alpha_old = lax.fori_loop(0, count - 1, iterate, (ones, ones))
        slot = (count - 1) % 2
        middle_sums(slot)
        gamma, delta = finish_sums(slot)
        alpha, beta = scalars(count - 1, gamma, delta, gamma_old, alpha_old)

        def last(x, _):
            for c in range(3):
                ubuf[c, x + 1, LO:HI, :] = ubuf[c, x + 1, LO:HI, :] + alpha * (r[c, x] + beta * p[c, x])
            return 0

        planes(last, 0)

    tall = jnp.zeros((NYL, NZL), f32)

    def close(x, carry):
        held, sums = carry
        for c in range(3):
            plane = ubuf[c, x + 1, LO:HI, :]
            vout[c, x] = plane
            held = pack(U_SET, c, x, plane, held)
            if c == 2:
                sums = jnp.where(lane_full == x, jnp.sum(plane, axis=1, keepdims=True), sums)
        return held, sums

    held, sums = planes(close, (no_pack, tall))
    zs[U_SET] = held
    start_faces(ubuf, U_SET, 3)
    square = jnp.concatenate([sums, jnp.zeros((NZL - NYL, NZL), f32)], axis=0)
    across = NZL // NYL
    flat = jnp.transpose(square)[0:NXL]
    tiles[place] = pltpu.roll(flat, lax.rem(my, across) * NYL, 1)

    def tile_copy(k):
        mine = tiles.at[place]
        return pltpu.make_async_remote_copy(
            src_ref=mine, dst_ref=mine, send_sem=tile_send.at[k], recv_sem=tile_recv.at[k],
            device_id=at_group(k), device_id_type=MESH,
        )

    for k in range(1, group):
        tile_copy(k).start()
    finish_faces(ubuf, U_SET, 3)
    u_rim = zr[U_SET]

    def harden(x, _):
        rate = rate_at(x, u_rim)
        plastic = jnp.maximum(rate - strength[x] / (2.0 * visc[x]), 0.0)
        sout[x] = strain[x] + strain_step * plastic
        return 0

    planes(harden, 0)
    for k in range(1, group):
        tile_copy(k).wait()
    scale = surface_step * uplift_gain / (pz * NZL)
    for part in range(py // across):
        total = tiles[part * across * pz]
        for k in range(1, across * pz):
            total = total + tiles[part * across * pz + k]
        span = slice(part * NZL, (part + 1) * NZL)
        tout[:, span] = base[:, span] + scale * total


def build(counts, ident, px, py, pz, name):
    field = (3, NXL, NYL, NZL)
    cell = (NXL, NYL, NZL)
    cols = py * NYL
    group = py * pz
    dma = pltpu.SemaphoreType.DMA
    vmem = pl.BlockSpec(memory_space=pltpu.VMEM)
    return pl.pallas_call(
        functools.partial(step_kernel, counts, px, py, pz),
        out_shape=[
            jax.ShapeDtypeStruct(field, f32),
            jax.ShapeDtypeStruct(cell, f32),
            jax.ShapeDtypeStruct((NXL, cols), f32),
        ],
        in_specs=[vmem] * 7,
        out_specs=[vmem] * 3,
        scratch_shapes=[
            pltpu.VMEM((3, NXL + 2, BUFY, NZL), f32),
            pltpu.VMEM((1, NXL + 2, BUFY, NZL), f32),
            pltpu.VMEM((2, 3, NXL + 2, BUFY, NZL), f32),
            pltpu.VMEM((4, 2, 3, NXL, NZL), f32),
            pltpu.VMEM((4, 2, 3, NXL, NZL), f32),
            pltpu.VMEM((4, NYL // 2, NZL), f32),
            pltpu.VMEM((4, NYL // 2, NZL), f32),
            pltpu.VMEM(cell, f32),
            pltpu.VMEM((7, *cell), f32),
            pltpu.VMEM(field, f32),
            pltpu.VMEM(field, f32),
            pltpu.VMEM(field, f32),
            pltpu.VMEM(field, f32),
            pltpu.VMEM(field, f32),
            pltpu.VMEM((2, px, 2, NZL), f32),
            pltpu.VMEM((2, group, 2, NZL), f32),
            pltpu.VMEM((2, NXL + 2 * RIM, cols), f32),
            pltpu.VMEM((NXL, cols), f32),
            pltpu.VMEM((group, NXL, NZL), f32),
            dma((4, 5)), dma((4, 5)),
            dma((2, px)), dma((2, px)),
            dma((2, group)), dma((2, group)),
            dma((2,)), dma((2,)),
            dma((group,)), dma((group,)),
        ],
        compiler_params=pltpu.CompilerParams(
            collective_id=ident, has_side_effects=True, vmem_limit_bytes=40 * 1024 * 1024
        ),
        name=name,
    )


def local(px, py, pz, force, vel, visc, strain, flags, counts, heights, receivers):
    long_first = build((KMAX, KMAX - 2), 0, px, py, pz, "long_first")
    short_first = build((KMAX - 2, KMAX), 1, px, py, pz, "short_first")
    args = (force, vel, visc, strain, flags, heights, receivers)
    out = lax.cond(counts[0] == KMAX, lambda *a: tuple(long_first(*a)), lambda *a: tuple(short_first(*a)), *args)
    return tuple(out)


def solution(mesh):
    px, py, pz = mesh.shape["mx"], mesh.shape["my"], mesh.shape["mz"]
    vector, scalar, rows = P(None, "mx", "my", "mz"), P("mx", "my", "mz"), P("mx", None)
    return jax.shard_map(
        functools.partial(local, px, py, pz),
        mesh=mesh,
        in_specs=(vector, vector, scalar, scalar, scalar, P(), rows, rows),
        out_specs=(vector, scalar, rows),
        check_vma=False,
    )
```

time: 1100 us -> 146 us (0.13); the launches traced: 1080 us -> 146 us
  starting transfers between devices: 384 us -> 0 us
  blocking collectives: 370 us -> 0 us
  local copies, waits for them, and re-layouts: 153 us -> 2.84 us
  Pallas kernels: 0 us -> 142 us
  other arithmetic: 125 us -> 0 us
  between operations: 49.7 us -> 0.69 us
    ppermute x106 -> x0, starting transfers between devices: 378 us -> none  [the longest x39 180 us: with_halo(): lax.ppermute(last, axis, up)]
    psum x60 -> x0, blocking collectives: 370 us -> none  [by_axis(): return functools.reduce(lax.psum, axes, array)]
    pallas_call x0 -> x1, Pallas kernels: none -> 142 us  [local(): short_first(*a)]
    slice x83 -> x0, local copies, waits for them, and re-layouts: 84.2 us -> none  [the longest x51 54 us: with_halo(): last = lax.slice_in_dim(array, length - width, length, axis=dim)]
    reduce_sum x16 -> x0, other arithmetic: 61.9 us -> none  [the longest x12 56.6 us: paired_products(): jnp.sum(residual * applied)]
    ppermute x34 -> x0, local copies, waits for them, and re-layouts: 39.2 us -> none  [the longest x13 18.3 us: with_halo(): lax.ppermute(last, axis, up)]
    sub x10 -> x0, other arithmetic: 18.6 us -> none  [the longest x8 15.3 us: krylov_solve(): residual = residual - stepped * along_applied]
    mul x12 -> x0, other arithmetic: 14.4 us -> none  [the longest x5 8.47 us: rate_invariant(): 0.5 * (neighbour(padded, dimension, 1) - neighbour(padded, dimension, -1))]
  transfers between devices with their start and end apart: 107 -> 0, of which waited for: 2 -> 0; matrix products, arithmetic and copies ran while one was open for 17% -> 0% of each run, Pallas kernels for 0% -> 0%
where the time goes in v1:
time: 146 us
  Pallas kernels  142 us (97%)
  local copies, waits for them, and re-layouts  2.84 us (2%)
    pallas_call x1, Pallas kernels, local(): short_first(*a)  142 us

profile of v1, /device:TPU:1, one launch (start us, length us, event | category | flops | bytes accessed | tf_op | source)
XLA Modules:
  0.0 145.8 jit_solution(3577702315825331949)
XLA Ops:
  0.6 0.0 copy-start
  0.6 0.6 copy-done
  1.3 142.3 %conditional.1 = ((f32[3,16,32,128]{3,2,1,0:T(8,128)S(1)}, f32[16,32,128]{2,1,0:T(8,128)S(1)}, f32[16,256]{1,0:T(8,128)S(1)})) conditional(s32[]{:T(128)} %bitcast, (f32[3,16,32,128]{3,2,1,0:T(8,128)}, f32[3,16,32,128]{3,2,1,0:T(8,128)}, f32[16,32,128]{2,1,0:T(8,128)}, f32[16,32,128]{2,1,0:T(8,128)}, s32[16,32,128]{2,1,0:T(8,128)}, ...), branch_computations={%region_0.0_spmd, %region_1.0_spmd} | conditional | bytes 8 | solution.py:547
  1.3 142.3 %short_first.1 = (f32[3,16,32,128]{3,2,1,0:T(8,128)S(1)}, f32[16,32,128]{2,1,0:T(8,128)S(1)}, f32[16,256]{1,0:T(8,128)S(1)}) custom-call(f32[3,16,32,128]{3,2,1,0:T(8,128)} %get-tuple-element.28.force, f32[3,16,32,128]{3,2,1,0:T(8,128)} %get-tuple-element.29.vel, f32[16,32,128]{2,1,0:T(8,128)} %get-tuple-element.30.visc, ...), custom_call_target="tpu_custom_call" | custom-call | tf_op jit(solution)/shard_map/cond/branch_0_fun/short_first/pallas_call | solution.py:547
  143.6 0.9 copy.26
  144.5 0.7 copy.27
  145.2 0.6 copy.28
Async XLA Ops:
  0.6 0.7 copy-start

commit v2 on v1

--- a/solution.py
+++ b/solution.py
@@ -31,15 +31,66 @@
 neighbour_steps = ((-1, -1), (-1, 0), (-1, 1), (0, -1), (0, 1), (1, -1), (1, 0), (1, 1))
 
 MESH = pl.DeviceIdType.MESH
-U_SET, E_SET = 2, 3
+U_SET, E_SET = KMAX, KMAX + 1
+CUT = 3
+ROWS = 32
 f32 = jnp.float32
+
+
+def lanczos(gram, top):
+    turn, norms = [], []
+    for i in range(top + 1):
+        row = [0.0] * i + [1.0]
+        for j in range(i):
+            part = gram[i, j]
+            for k in range(j):
+                part = part + turn[j][k] * gram[i, k]
+            part = part / norms[j]
+            for k in range(j + 1):
+                row[k] = row[k] - part * turn[j][k]
+        norm = gram[i, i]
+        for k in range(i):
+            norm = norm + row[k] * gram[i, k]
+        turn.append(row)
+        norms.append(norm)
+    return turn, norms
+
+
+def solve(gram, shift, n):
+    lower, pivots, right = {}, [], []
+
+    def entry(i, j):
+        total = gram[i, j + 1]
+        for m, part in shift[j].items():
+            total = total + part * gram[i, m]
+        return total
+
+    for i in range(n):
+        for j in range(i):
+            part = entry(i, j)
+            for k in range(j):
+                part = part - lower[i, k] * lower[j, k] * pivots[k]
+            lower[i, j] = part / pivots[j]
+        pivot = entry(i, i)
+        for k in range(i):
+            pivot = pivot - lower[i, k] * lower[i, k] * pivots[k]
+        pivots.append(pivot)
+        part = gram[i, 0]
+        for k in range(i):
+            part = part - lower[i, k] * right[k]
+        right.append(part)
+    steps = [part / pivot for part, pivot in zip(right, pivots)]
+    for i in reversed(range(n)):
+        for k in range(i + 1, n):
+            steps[i] = steps[i] - lower[k, i] * steps[k]
+    return steps
 
 
 def step_kernel(
     counts, px, py, pz,
     force, vel, visc, strain, flags, heights, receivers,
     vout, sout, tout,
-    ubuf, ebuf, wbuf, ys, yr, zs, zr, strength, coef, r, p, s, z, q, sums1, sums2, surf, base, tiles,
+    ubuf, ebuf, bbuf, ys, yr, zs, zr, strength, coef, dots, sums1, sums2, surf, base, tiles,
     face_send, face_recv, one_send, one_recv, two_send, two_recv, surf_send, surf_recv, tile_send, tile_recv,
 ):
     mx, my, mz = lax.axis_index("mx"), lax.axis_index("my"), lax.axis_index("mz")
@@ -74,9 +125,10 @@
 
     blank(ubuf, 3)
     blank(ebuf, 1)
-    blank(wbuf.at[0], 3)
-    blank(wbuf.at[1], 3)
-    for kind in range(4):
+    for k in range(KMAX):
+        blank(bbuf.at[k], 3)
+    dots[...] = jnp.zeros(dots.shape, f32)
+    for kind in range(KMAX + 2):
         for side in range(2):
             for c in range(3):
                 yr[kind, side, c] = jnp.zeros((NXL, NZL), f32)
@@ -129,6 +181,8 @@
             def _():
                 face_copy(kind, d, src, dst, device).wait_recv()
         depth_copy(kind).wait()
+
+    def spread_rows(buf, kind, n):
         for c in range(n):
             low, high = yr[kind, 0, c], yr[kind, 1, c]
             for x in range(NXL):
@@ -204,10 +258,10 @@
             device_id=at_group(k), device_id_type=MESH,
         )
 
-    def start_sums(slot, gg, dd):
-        sums1[slot, mx] = jnp.concatenate(
-            [jnp.sum(gg, axis=0, keepdims=True), jnp.sum(dd, axis=0, keepdims=True)], axis=0
-        )
+    def start_sums(slot, bank):
+        spot = lax.broadcasted_iota(jnp.int32, (ROWS, NZL), 0) == lanes(ROWS)
+        line = jnp.sum(dots[bank], axis=1, keepdims=True)
+        sums1[slot, mx] = jnp.sum(jnp.where(spot, line, 0.0), axis=0, keepdims=True)
         for k in range(1, px):
             one_copy(slot, k).start()
 
@@ -218,12 +272,56 @@
         for k in range(1, group):
             two_copy(slot, k).start()
 
-    def finish_sums(slot):
+    def finish_sums(slot, names, gram):
         for k in range(1, group):
             two_copy(slot, k).wait()
-        both = jnp.sum(jnp.sum(sums2[slot], axis=0), axis=1, keepdims=True)
-        both = jnp.broadcast_to(both, (2, NZL))
-        return both[0:1], both[1:2]
+        total = jnp.sum(sums2[slot], axis=0)
+        for spot, (i, j) in enumerate(names):
+            gram[i, j] = gram[j, i] = jnp.broadcast_to(total[:, spot : spot + 1], (1, NZL))
+
+    def fold(product):
+        return (product[0:8] + product[8:16]) + (product[16:24] + product[24:32])
+
+    def keep_dots(bank, names, pairs, sums):
+        for pair, total in zip(pairs, sums):
+            spot = len(names)
+            dots[bank, spot : spot + 1, :] = jnp.sum(total, axis=0, keepdims=True)
+            names.append(pair)
+
+    def straighten(mix, names):
+        pairs = [(m, CUT) for m in range(CUT + 1)]
+        for rim_of in (0, NXL + 1):
+            for c in range(3):
+                plane = bbuf[CUT, c, rim_of, LO:HI, :]
+                for m in range(CUT):
+                    plane = plane - mix[m] * bbuf[m, c, rim_of, LO:HI, :]
+                bbuf[CUT, c, rim_of, LO:HI, :] = plane
+        for side in range(2):
+            for c in range(3):
+                face = yr[CUT, side, c]
+                for m in range(CUT):
+                    face = face - mix[m] * yr[m, side, c]
+                yr[CUT, side, c] = face
+        face = zr[CUT]
+        for m in range(CUT):
+            face = face - mix[m] * zr[m]
+        zr[CUT] = face
+
+        def one(x, sums):
+            sums = list(sums)
+            for c in range(3):
+                own = [bbuf[m, c, x + 1, LO:HI, :] for m in range(CUT)]
+                plane = bbuf[CUT, c, x + 1, LO:HI, :]
+                for m in range(CUT):
+                    plane = plane - mix[m] * own[m]
+                bbuf[CUT, c, x + 1, LO:HI, :] = plane
+                own.append(plane)
+                for m in range(CUT + 1):
+                    sums[m] = sums[m] + fold(own[m] * plane)
+            return tuple(sums)
+
+        sums = planes(one, tuple(jnp.zeros((8, NZL), f32) for _ in range(CUT + 1)))
+        keep_dots(1, names, pairs, sums)
 
     def load(x, held):
         for c in range(3):
@@ -257,11 +355,6 @@
     def strengthen(x, _):
         weak = flags[x].astype(f32) * jnp.minimum(strain[x] / critical_strain, 1.0)
         strength[x] = cohesion_base * (1.0 - weakening * weak) * cos_friction + pressure * sin_friction
-        for c in range(3):
-            zero = jnp.zeros((NYL, NZL), f32)
-            p[c, x] = zero
-            s[c, x] = zero
-            z[c, x] = zero
         return 0
 
     planes(strengthen, 0)
@@ -309,16 +402,10 @@
     ground = height - (surface_step * erodibility) * jnp.sqrt(drained) * slope
     base[...] = ground[RIM : RIM + NXL]
 
+    none = jnp.zeros((8, NZL), f32)
+    finish_faces(ubuf, U_SET, 3)
+    spread_rows(ubuf, U_SET, 3)
     for picard, count in enumerate(counts):
-        if picard:
-            def resend(x, held):
-                for c in range(3):
-                    held = pack(U_SET, c, x, ubuf[c, x + 1, LO:HI, :], held)
-                return held
-
-            zs[U_SET] = planes(resend, no_pack)
-            start_faces(ubuf, U_SET, 3)
-        finish_faces(ubuf, U_SET, 3)
         u_rim = zr[U_SET]
 
         def soften(x, held):
@@ -330,9 +417,14 @@
         zs[E_SET] = planes(soften, no_pack)
         start_faces(ebuf, E_SET, 1)
         finish_faces(ebuf, E_SET, 1)
+        spread_rows(ebuf, E_SET, 1)
         e_rim = zr[E_SET]
-
-        def begin(x, held):
+        lagged = count <= CUT + 1
+        gram, rows_of = {}, ([], [])
+        shift = {}
+
+        def begin(x, carry):
+            held, norm = carry
             eta, pairs = around(ebuf, e_rim, 0, x)
             total = jnp.full((NYL, NZL), drag_coef, f32)
             for d in range(3):
@@ -344,118 +436,124 @@
             for c in range(3):
                 _, au = applied(ubuf, u_rim, c, x)
                 plane = force[c, x] - au
-                r[c, x] = plane
-                wbuf[0, c, x + 1, LO:HI, :] = plane
+                bbuf[0, c, x + 1, LO:HI, :] = plane
+                norm = norm + fold(plane * plane)
                 held = pack(0, c, x, plane, held)
-            return held
-
-        zs[0] = planes(begin, no_pack, 1)
-        start_faces(wbuf.at[0], 0, 3)
-        finish_faces(wbuf.at[0], 0, 3)
-        r_rim = zr[0]
-        nothing = jnp.zeros((NYL, NZL), f32)
-
-        def first(x, carry):
-            held, gg, dd = carry
-            for c in range(3):
-                v, w = applied(wbuf.at[0], r_rim, c, x)
-                wbuf[1, c, x + 1, LO:HI, :] = w
-                gg = gg + v * v
-                dd = dd + v * w
-                held = pack(1, c, x, w, held)
-            return held, gg, dd
-
-        held, gg, dd = planes(first, (no_pack, nothing, nothing))
-        zs[1] = held
-        start_sums(0, gg, dd)
-        start_faces(wbuf.at[1], 1, 3)
-
-        def scalars(i, gamma, delta, gamma_old, alpha_old):
-            beta = jnp.where(i == 0, 0.0, gamma / gamma_old)
-            alpha = gamma / (delta - beta * gamma / alpha_old)
-            return alpha, beta
-
-        def iterate(i, carry):
-            gamma_old, alpha_old = carry
-            now, later = lax.rem(i + 1, 2), lax.rem(i, 2)
-            w_now, w_later = wbuf.at[now], wbuf.at[later]
-            slot = lax.rem(i, 2)
-            middle_sums(slot)
-            finish_faces(w_now, now, 3)
-            rim = zr[now]
-
-            def again(x, _):
+            return held, norm
+
+        held, norm = planes(begin, (no_pack, none), 1)
+        zs[0] = held
+        keep_dots(0, rows_of[0], [(0, 0)], [norm])
+        start_faces(bbuf.at[0], 0, 3)
+        early = 2 * picard
+        for k in range(count):
+            if k != CUT:
+                finish_faces(bbuf.at[k], k, 3)
+                spread_rows(bbuf.at[k], k, 3)
+            if lagged and k == CUT - 1:
+                middle_sums(early)
+            rim = zr[k]
+            stored = k + 1 < count
+            extra = {}
+            if k >= CUT:
+                extra[k] = alpha
+                if k == CUT:
+                    for m in range(CUT):
+                        extra[m] = beta * turn[CUT - 1][m]
+                else:
+                    extra[k - 1] = beta
+            partners = [m for m in range(k + 2 if stored else k + 1)]
+            if k + 1 == CUT and lagged:
+                partners = []
+
+            def grow(x, carry):
+                held, sums = carry
+                sums = list(sums)
                 for c in range(3):
-                    q[c, x] = applied(w_now, rim, c, x)[1]
-                return 0
-
-            planes(again, 0)
-            gamma, delta = finish_sums(slot)
-            alpha, beta = scalars(i, gamma, delta, gamma_old, alpha_old)
-
-            def update(x, carry):
-                held, gg, dd = carry
-                for c in range(3):
-                    w = w_now[c, x + 1, LO:HI, :]
-                    z_new = q[c, x] + beta * z[c, x]
-                    s_new = w + beta * s[c, x]
-                    r_old = r[c, x]
-                    p_new = r_old + beta * p[c, x]
-                    r_new = r_old - alpha * s_new
-                    w_new = w - alpha * z_new
-                    z[c, x] = z_new
-                    s[c, x] = s_new
-                    p[c, x] = p_new
-                    r[c, x] = r_new
-                    w_later[c, x + 1, LO:HI, :] = w_new
-                    ubuf[c, x + 1, LO:HI, :] = ubuf[c, x + 1, LO:HI, :] + alpha * p_new
-                    gg = gg + r_new * r_new
-                    dd = dd + r_new * w_new
-                    held = pack(later, c, x, w_new, held)
-                return held, gg, dd
-
-            held, gg, dd = planes(update, (no_pack, nothing, nothing))
-            zs[later] = held
-            start_sums(later_slot(i), gg, dd)
-
-            @pl.when(i < count - 2)
-            def _():
-                start_faces(w_later, later, 3)
-
-            return gamma, alpha
-
-        def later_slot(i):
-            return lax.rem(i + 1, 2)
-
-        ones = jnp.ones((1, NZL), f32)
-        gamma_old, alpha_old = lax.fori_loop(0, count - 1, iterate, (ones, ones))
-        slot = (count - 1) % 2
-        middle_sums(slot)
-        gamma, delta = finish_sums(slot)
-        alpha, beta = scalars(count - 1, gamma, delta, gamma_old, alpha_old)
-
-        def last(x, _):
-            for c in range(3):
-                ubuf[c, x + 1, LO:HI, :] = ubuf[c, x + 1, LO:HI, :] + alpha * (r[c, x] + beta * p[c, x])
-            return 0
-
-        planes(last, 0)
-
-    tall = jnp.zeros((NYL, NZL), f32)
-
-    def close(x, carry):
-        held, sums = carry
-        for c in range(3):
-            plane = ubuf[c, x + 1, LO:HI, :]
-            vout[c, x] = plane
-            held = pack(U_SET, c, x, plane, held)
-            if c == 2:
-                sums = jnp.where(lane_full == x, jnp.sum(plane, axis=1, keepdims=True), sums)
-        return held, sums
-
-    held, sums = planes(close, (no_pack, tall))
-    zs[U_SET] = held
-    start_faces(ubuf, U_SET, 3)
+                    v, w = applied(bbuf.at[k], rim, c, x)
+                    own = {}
+                    for m in set(extra) | set(partners):
+                        if m <= k:
+                            own[m] = v if m == k else bbuf[m, c, x + 1, LO:HI, :]
+                    for m in sorted(extra):
+                        w = w - extra[m] * own[m]
+                    own[k + 1] = w
+                    if stored:
+                        bbuf[k + 1, c, x + 1, LO:HI, :] = w
+                        held = pack(k + 1, c, x, w, held)
+                    for at, m in enumerate(partners):
+                        sums[at] = sums[at] + fold(own[m] * w)
+                return held, tuple(sums)
+
+            held, sums = planes(grow, (no_pack, tuple(none for _ in partners)))
+            shift[k] = dict(extra)
+            bank = 0 if k + 1 < CUT or (k + 1 == CUT and not lagged) else 1
+            keep_dots(bank, rows_of[bank], [(m, k + 1) for m in partners], sums)
+            if k + 1 == (CUT - 1 if lagged else CUT):
+                start_sums(early, 0)
+            if stored:
+                zs[k + 1] = held
+                start_faces(bbuf.at[k + 1], k + 1, 3)
+            if k + 1 == CUT:
+                if not lagged:
+                    middle_sums(early)
+                finish_faces(bbuf.at[CUT], CUT, 3)
+                finish_sums(early, rows_of[0], gram)
+                turn, norms = lanczos(gram, CUT - 1 if lagged else CUT)
+                top = CUT - 1 if lagged else CUT
+                beta = norms[top] / norms[top - 1]
+                alpha = turn[top - 1][top - 2] - turn[top][top - 1]
+                if lagged:
+                    full = [0.0] * (CUT + 1)
+                    for m in range(CUT):
+                        full[m + 1] = full[m + 1] + turn[top][m]
+                        full[m] = full[m] - alpha * turn[top][m]
+                    for m in range(CUT - 1):
+                        full[m] = full[m] - beta * turn[top - 1][m]
+                    mix = [-full[m] for m in range(CUT)]
+                else:
+                    mix = [-turn[CUT][m] for m in range(CUT)]
+                shift[CUT - 1] = dict(enumerate(mix))
+                straighten(mix, rows_of[1])
+                spread_rows(bbuf.at[CUT], CUT, 3)
+
+        start_sums(early + 1, 1)
+        middle_sums(early + 1)
+        finish_sums(early + 1, rows_of[1], gram)
+        steps = solve(gram, shift, count)
+        final = picard == len(counts) - 1
+        tall = jnp.zeros((NYL, NZL), f32)
+
+        def total_of(first, parts):
+            for step, part in zip(steps, parts):
+                first = first + step * part
+            return first
+
+        for rim_of in (0, NXL + 1):
+            for c in range(3):
+                ubuf[c, rim_of, LO:HI, :] = total_of(
+                    ubuf[c, rim_of, LO:HI, :], [bbuf[m, c, rim_of, LO:HI, :] for m in range(count)]
+                )
+        for side in range(2):
+            for c in range(3):
+                yr[U_SET, side, c] = total_of(yr[U_SET, side, c], [yr[m, side, c] for m in range(count)])
+        zr[U_SET] = total_of(zr[U_SET], [zr[m] for m in range(count)])
+
+        def settle(x, sums):
+            for c in range(3):
+                plane = total_of(
+                    ubuf[c, x + 1, LO:HI, :], [bbuf[m, c, x + 1, LO:HI, :] for m in range(count)]
+                )
+                ubuf[c, x + 1, LO:HI, :] = plane
+                if final:
+                    vout[c, x] = plane
+                    if c == 2:
+                        sums = jnp.where(lane_full == x, jnp.sum(plane, axis=1, keepdims=True), sums)
+            return sums
+
+        sums = planes(settle, tall)
+        spread_rows(ubuf, U_SET, 3)
+
     square = jnp.concatenate([sums, jnp.zeros((NZL - NYL, NZL), f32)], axis=0)
     across = NZL // NYL
     flat = jnp.transpose(square)[0:NXL]
@@ -470,7 +568,6 @@
 
     for k in range(1, group):
         tile_copy(k).start()
-    finish_faces(ubuf, U_SET, 3)
     u_rim = zr[U_SET]
 
     def harden(x, _):
@@ -510,26 +607,22 @@
         scratch_shapes=[
             pltpu.VMEM((3, NXL + 2, BUFY, NZL), f32),
             pltpu.VMEM((1, NXL + 2, BUFY, NZL), f32),
-            pltpu.VMEM((2, 3, NXL + 2, BUFY, NZL), f32),
-            pltpu.VMEM((4, 2, 3, NXL, NZL), f32),
-            pltpu.VMEM((4, 2, 3, NXL, NZL), f32),
-            pltpu.VMEM((4, NYL // 2, NZL), f32),
-            pltpu.VMEM((4, NYL // 2, NZL), f32),
+            pltpu.VMEM((KMAX, 3, NXL + 2, BUFY, NZL), f32),
+            pltpu.VMEM((KMAX + 2, 2, 3, NXL, NZL), f32),
+            pltpu.VMEM((KMAX + 2, 2, 3, NXL, NZL), f32),
+            pltpu.VMEM((KMAX + 2, NYL // 2, NZL), f32),
+            pltpu.VMEM((KMAX + 2, NYL // 2, NZL), f32),
             pltpu.VMEM(cell, f32),
             pltpu.VMEM((7, *cell), f32),
-            pltpu.VMEM(field, f32),
-            pltpu.VMEM(field, f32),
-            pltpu.VMEM(field, f32),
-            pltpu.VMEM(field, f32),
-            pltpu.VMEM(field, f32),
-            pltpu.VMEM((2, px, 2, NZL), f32),
-            pltpu.VMEM((2, group, 2, NZL), f32),
+            pltpu.VMEM((2, ROWS, NZL), f32),
+            pltpu.VMEM((4, px, 1, NZL), f32),
+            pltpu.VMEM((4, group, 1, NZL), f32),
             pltpu.VMEM((2, NXL + 2 * RIM, cols), f32),
             pltpu.VMEM((NXL, cols), f32),
             pltpu.VMEM((group, NXL, NZL), f32),
-            dma((4, 5)), dma((4, 5)),
-            dma((2, px)), dma((2, px)),
-            dma((2, group)), dma((2, group)),
+            dma((KMAX + 2, 5)), dma((KMAX + 2, 5)),
+            dma((4, px)), dma((4, px)),
+            dma((4, group)), dma((4, group)),
             dma((2,)), dma((2,)),
             dma((group,)), dma((group,)),
         ],

time: 146 us -> 119 us (0.82)
  Pallas kernels: 142 us -> 114 us
    pallas_call x1, Pallas kernels: 142 us -> 114 us  [local(): long_first(*a)]
where the time goes in v2:
time: 119 us; the launch traced here: 118 us
  Pallas kernels  114 us (96%)
  local copies, waits for them, and re-layouts  2.84 us (2%)
    pallas_call x1, Pallas kernels, local(): long_first(*a)  114 us
    unnamed x5, local copies, waits for them, and re-layouts  2.84 us

profile of v2, /device:TPU:1, one launch (start us, length us, event | category | flops | bytes accessed | tf_op | source)
XLA Modules:
  0.0 117.7 jit_solution(3641711739329503711)
XLA Ops:
  0.6 0.0 copy-start
  0.6 0.6 copy-done
  1.3 114.2 %conditional.1 = ((f32[3,16,32,128]{3,2,1,0:T(8,128)S(1)}, f32[16,32,128]{2,1,0:T(8,128)S(1)}, f32[16,256]{1,0:T(8,128)S(1)})) conditional(s32[]{:T(128)} %bitcast, (f32[3,16,32,128]{3,2,1,0:T(8,128)}, f32[3,16,32,128]{3,2,1,0:T(8,128)}, f32[16,32,128]{2,1,0:T(8,128)}, f32[16,32,128]{2,1,0:T(8,128)}, s32[16,32,128]{2,1,0:T(8,128)}, ...), branch_computations={%region_0.0_spmd, %region_1.0_spmd} | conditional | bytes 8 | solution.py:640
  1.5 114.0 %long_first.1 = (f32[3,16,32,128]{3,2,1,0:T(8,128)S(1)}, f32[16,32,128]{2,1,0:T(8,128)S(1)}, f32[16,256]{1,0:T(8,128)S(1)}) custom-call(f32[3,16,32,128]{3,2,1,0:T(8,128)} %get-tuple-element.35.force, f32[3,16,32,128]{3,2,1,0:T(8,128)} %get-tuple-element.36.vel, f32[16,32,128]{2,1,0:T(8,128)} %get-tuple-element.37.visc, ...), custom_call_target="tpu_custom_call" | custom-call | tf_op jit(solution)/shard_map/cond/branch_1_fun/long_first/pallas_call | solution.py:640
  115.5 0.9 copy.26
  116.4 0.7 copy.27
  117.1 0.6 copy.28
Async XLA Ops:
  0.6 0.7 copy-start

commit v3 on v2

--- a/solution.py
+++ b/solution.py
@@ -88,8 +88,9 @@
 
 def step_kernel(
     counts, px, py, pz,
-    force, vel, visc, strain, flags, heights, receivers,
+    force_in, vel_in, visc_in, strain_in, flags_in, heights_in, receivers_in,
     vout, sout, tout,
+    force, visc, strain, flags, heights, receivers, load_sem,
     ubuf, ebuf, bbuf, ys, yr, zs, zr, strength, coef, dots, sums1, sums2, surf, base, tiles,
     face_send, face_recv, one_send, one_recv, two_send, two_recv, surf_send, surf_recv, tile_send, tile_recv,
 ):
@@ -123,22 +124,38 @@
             buf[c, 0, LO:HI, :] = zero
             buf[c, NXL + 1, LO:HI, :] = zero
 
+    loads = [
+        pltpu.make_async_copy(src, dst, load_sem.at[k])
+        for k, (src, dst) in enumerate((
+            (vel_in, ubuf.at[:, 1 : NXL + 1, LO:HI, :]), (heights_in, heights), (receivers_in, receivers),
+            (strain_in, strain), (flags_in, flags), (visc_in, visc), (force_in, force),
+        ))
+    ]
+    for copy in loads:
+        copy.start()
+
     blank(ubuf, 3)
     blank(ebuf, 1)
-    for k in range(KMAX):
+
+    def blank_one(k, _):
         blank(bbuf.at[k], 3)
+        return 0
+
+    lax.fori_loop(0, KMAX, blank_one, 0)
     dots[...] = jnp.zeros(dots.shape, f32)
-    for kind in range(KMAX + 2):
+
+    def blank_rows(kind, _):
         for side in range(2):
             for c in range(3):
                 yr[kind, side, c] = jnp.zeros((NXL, NZL), f32)
+        return 0
+
+    lax.fori_loop(0, KMAX + 2, blank_rows, 0)
     rows, cols = surf.shape[1:]
     surf[0, 0:RIM, :] = jnp.full((RIM, cols), -1.0, f32)
     surf[0, RIM + NXL :, :] = jnp.full((RIM, cols), -1.0, f32)
     surf[1, 0:RIM, :] = jnp.zeros((RIM, cols), f32)
     surf[1, RIM + NXL :, :] = jnp.zeros((RIM, cols), f32)
-    surf[0, RIM : RIM + NXL, :] = receivers[...].astype(f32)
-    surf[1, RIM : RIM + NXL, :] = heights[...]
 
     barrier = pltpu.get_barrier_semaphore()
     for k in range(1, px):
@@ -146,9 +163,11 @@
     for k in range(1, group):
         pl.semaphore_signal(barrier, inc=1, device_id=at_group(k), device_id_type=MESH)
 
-    def face_copy(kind, d, src, dst, device):
+    turn_of = {"start": 0, "finish": 0}
+
+    def face_copy(turn, d, src, dst, device):
         return pltpu.make_async_remote_copy(
-            src_ref=src, dst_ref=dst, send_sem=face_send.at[kind, d], recv_sem=face_recv.at[kind, d],
+            src_ref=src, dst_ref=dst, send_sem=face_send.at[d], recv_sem=face_recv.at[turn, d],
             device_id=device, device_id_type=MESH,
         )
 
@@ -161,79 +180,96 @@
             (my > 0, my < py - 1, 3, ys.at[kind, 0, comps], yr.at[kind, 1, comps], {"my": my - 1}),
         )
 
-    def depth_copy(kind):
-        return face_copy(kind, 4, zs.at[kind], zr.at[kind], {"mz": 1 - mz})
+    def depth_copy(turn, kind):
+        return face_copy(turn, 4, zs.at[kind], zr.at[kind], {"mz": 1 - mz})
 
     def start_faces(buf, kind, n):
-        depth_copy(kind).start()
+        turn = turn_of["start"] % 2
+        turn_of["start"] += 1
+        depth_copy(turn, kind).start()
         for sends, _, d, src, dst, device in face_copies(buf, kind, n):
             @pl.when(sends)
             def _():
-                face_copy(kind, d, src, dst, device).start()
+                face_copy(turn, d, src, dst, device).start()
 
     def finish_faces(buf, kind, n):
+        turn = turn_of["finish"] % 2
+        turn_of["finish"] += 1
         for sends, receives, d, src, dst, device in face_copies(buf, kind, n):
             @pl.when(sends)
             def _():
-                face_copy(kind, d, src, dst, device).wait_send()
+                face_copy(turn, d, src, dst, device).wait_send()
 
             @pl.when(receives)
             def _():
-                face_copy(kind, d, src, dst, device).wait_recv()
-        depth_copy(kind).wait()
+                face_copy(turn, d, src, dst, device).wait_recv()
+        depth_copy(turn, kind).wait()
 
     def spread_rows(buf, kind, n):
-        for c in range(n):
-            low, high = yr[kind, 0, c], yr[kind, 1, c]
-            for x in range(NXL):
-                buf[c, x + 1, LO - 1 : LO, :] = low[x : x + 1]
-                buf[c, x + 1, HI : HI + 1, :] = high[x : x + 1]
-
-    half = NYL // 2
-    lane_half = lanes(half)
+        def spread(x, _):
+            for c in range(n):
+                buf[c, x + 1, LO - 1 : LO, :] = yr[kind, 0, c, pl.ds(x, 1), :]
+                buf[c, x + 1, HI : HI + 1, :] = yr[kind, 1, c, pl.ds(x, 1), :]
+            return 0
+
+        lax.fori_loop(0, NXL, spread, 0, unroll=4)
+
     lane_full = lanes(NYL)
-
-    def pack(kind, c, x, plane, held):
-        ys[kind, 0, c, pl.ds(x, 1), :] = plane[0:1]
-        ys[kind, 1, c, pl.ds(x, 1), :] = plane[NYL - 1 :]
-        for part in range(2):
-            spot = c * NXL + x + 48 * part
-            turned = pltpu.roll(plane[part * half : (part + 1) * half], lax.rem(spot - edge + NZL, NZL), 1)
-            held = jnp.where(lane_half == spot, turned, held)
-        return held
-
-    no_pack = jnp.zeros((half, NZL), f32)
-
-    def depth_pair(v, arrived, c, x):
-        parts = []
-        for part in range(2):
-            spot = c * NXL + x + 48 * part
-            parts.append(pltpu.roll(arrived, lax.rem(edge - spot + NZL, NZL), 1))
-        rim = jnp.where(lane_full == edge, jnp.concatenate(parts, axis=0), 0.0)
-        below = jnp.where(lane_full == 0, rim, pltpu.roll(v, 1, 1))
-        above = jnp.where(lane_full == NZL - 1, rim, pltpu.roll(v, NZL - 1, 1))
-        return below, above
-
-    def around(buf, arrived, c, x):
-        v = buf[c, x + 1, LO:HI, :]
-        below, above = depth_pair(v, arrived, c, x)
+    lane_tile = lanes(8)
+    tiles_in = range(NYL // 8)
+
+    def at(t, step=0):
+        return slice(LO + 8 * t + step, LO + 8 * t + step + 8)
+
+    def own(t):
+        return slice(8 * t, 8 * t + 8)
+
+    def pack(kind, c, x, t, tile, held):
+        if t == 0:
+            ys[kind, 0, c, pl.ds(x, 1), :] = tile[0:1]
+        if t == NYL // 8 - 1:
+            ys[kind, 1, c, pl.ds(x, 1), :] = tile[7:8]
+        spot = c * NXL + x + 48 * (t // 2)
+        turned = pltpu.roll(tile, spot - edge + NZL, 1)
+        held = list(held)
+        held[t % 2] = jnp.where(lane_tile == spot, turned, held[t % 2])
+        return tuple(held)
+
+    none = jnp.zeros((8, NZL), f32)
+    no_pack = (none, none)
+
+    def keep_pack(kind, held):
+        zs[kind, 0:8] = held[0]
+        zs[kind, 8:16] = held[1]
+
+    def turned_rim(kind, c, x, t):
+        spot = c * NXL + x + 48 * (t // 2)
+        return pltpu.roll(zr[kind, own(t % 2)], edge - spot + NZL, 1)
+
+    def around(buf, kind, c, x, t):
+        v = buf[c, x + 1, at(t), :]
+        rim = jnp.where(lane_tile == edge, turned_rim(kind, c, x, t), 0.0)
+        below = jnp.where(lane_tile == 0, rim, pltpu.roll(v, 1, 1))
+        above = jnp.where(lane_tile == NZL - 1, rim, pltpu.roll(v, NZL - 1, 1))
         return v, (
-            (buf[c, x, LO:HI, :], buf[c, x + 2, LO:HI, :]),
-            (buf[c, x + 1, LO - 1 : HI - 1, :], buf[c, x + 1, LO + 1 : HI + 1, :]),
+            (buf[c, x, at(t), :], buf[c, x + 2, at(t), :]),
+            (buf[c, x + 1, at(t, -1), :], buf[c, x + 1, at(t, 1), :]),
             (below, above),
         )
 
-    def applied(buf, arrived, c, x):
-        v, pairs = around(buf, arrived, c, x)
-        total = coef[6, x] * v
-        for d in range(3):
-            total = total - coef[2 * d, x] * pairs[d][0] - coef[2 * d + 1, x] * pairs[d][1]
-        return v, total
-
-    def rate_at(x, arrived):
+    def applied(buf, kind, c, x, t):
+        v = buf[c, x + 1, at(t), :]
+        total = coef[6, x, own(t)] * v
+        total = total - coef[0, x, own(t)] * buf[c, x, at(t), :] - coef[1, x, own(t)] * buf[c, x + 2, at(t), :]
+        total = total - coef[2, x, own(t)] * buf[c, x + 1, at(t, -1), :]
+        total = total - coef[3, x, own(t)] * buf[c, x + 1, at(t, 1), :]
+        total = total - coef[4, x, own(t)] * pltpu.roll(v, 1, 1) - coef[5, x, own(t)] * pltpu.roll(v, NZL - 1, 1)
+        return v, total - coef[7, x, own(t)] * turned_rim(kind, c, x, t)
+
+    def rate_at(x, t):
         g = []
         for c in range(3):
-            _, pairs = around(ubuf, arrived, c, x)
+            _, pairs = around(ubuf, U_SET, c, x, t)
             g.append([0.5 * (pair[1] - pair[0]) for pair in pairs])
         total = g[0][0] * g[0][0] + g[1][1] * g[1][1] + g[2][2] * g[2][2]
         for a, b in ((0, 1), (0, 2), (1, 2)):
@@ -244,43 +280,36 @@
     def planes(body, carry, unroll=2):
         return lax.fori_loop(0, NXL, body, carry, unroll=unroll)
 
-    def one_copy(slot, k):
-        mine = sums1.at[slot, mx]
+    def sum_copy(sums, slot, mine, send, recv, device):
+        ref = sums.at[slot, mine]
         return pltpu.make_async_remote_copy(
-            src_ref=mine, dst_ref=mine, send_sem=one_send.at[slot, k], recv_sem=one_recv.at[slot, k],
-            device_id=at_row(k), device_id_type=MESH,
+            src_ref=ref, dst_ref=ref, send_sem=send, recv_sem=recv, device_id=device, device_id_type=MESH
         )
 
-    def two_copy(slot, k):
-        mine = sums2.at[slot, place]
-        return pltpu.make_async_remote_copy(
-            src_ref=mine, dst_ref=mine, send_sem=two_send.at[slot, k], recv_sem=two_recv.at[slot, k],
-            device_id=at_group(k), device_id_type=MESH,
-        )
+    def one_copy(slot, mine, k):
+        return sum_copy(sums1, slot, mine, one_send.at[0], one_recv.at[slot % 2], at_row(k))
+
+    def two_copy(slot, mine, k):
+        return sum_copy(sums2, slot, mine, two_send.at[0], two_recv.at[slot % 2], at_group(k))
 
     def start_sums(slot, bank):
         spot = lax.broadcasted_iota(jnp.int32, (ROWS, NZL), 0) == lanes(ROWS)
         line = jnp.sum(dots[bank], axis=1, keepdims=True)
         sums1[slot, mx] = jnp.sum(jnp.where(spot, line, 0.0), axis=0, keepdims=True)
         for k in range(1, px):
-            one_copy(slot, k).start()
+            one_copy(slot, mx, k).start()
 
     def middle_sums(slot):
-        for k in range(1, px):
-            one_copy(slot, k).wait()
+        one_copy(slot, slice(0, px - 1), 1).wait()
         sums2[slot, place] = jnp.sum(sums1[slot], axis=0)
         for k in range(1, group):
-            two_copy(slot, k).start()
+            two_copy(slot, place, k).start()
 
     def finish_sums(slot, names, gram):
-        for k in range(1, group):
-            two_copy(slot, k).wait()
+        two_copy(slot, slice(0, group - 1), 1).wait()
         total = jnp.sum(sums2[slot], axis=0)
         for spot, (i, j) in enumerate(names):
             gram[i, j] = gram[j, i] = jnp.broadcast_to(total[:, spot : spot + 1], (1, NZL))
-
-    def fold(product):
-        return (product[0:8] + product[8:16]) + (product[16:24] + product[24:32])
 
     def keep_dots(bank, names, pairs, sums):
         for pair, total in zip(pairs, sums):
@@ -309,28 +338,55 @@
 
         def one(x, sums):
             sums = list(sums)
-            for c in range(3):
-                own = [bbuf[m, c, x + 1, LO:HI, :] for m in range(CUT)]
-                plane = bbuf[CUT, c, x + 1, LO:HI, :]
-                for m in range(CUT):
-                    plane = plane - mix[m] * own[m]
-                bbuf[CUT, c, x + 1, LO:HI, :] = plane
-                own.append(plane)
-                for m in range(CUT + 1):
-                    sums[m] = sums[m] + fold(own[m] * plane)
+            for t in tiles_in:
+                for c in range(3):
+                    mine = [bbuf[m, c, x + 1, at(t), :] for m in range(CUT)]
+                    tile = bbuf[CUT, c, x + 1, at(t), :]
+                    for m in range(CUT):
+                        tile = tile - mix[m] * mine[m]
+                    bbuf[CUT, c, x + 1, at(t), :] = tile
+                    mine.append(tile)
+                    for m in range(CUT + 1):
+                        sums[m] = sums[m] + mine[m] * tile
             return tuple(sums)
 
-        sums = planes(one, tuple(jnp.zeros((8, NZL), f32) for _ in range(CUT + 1)))
+        sums = planes(one, (none,) * (CUT + 1))
         keep_dots(1, names, pairs, sums)
+
+    across = NZL // NYL
+
+    def tile_copy(mine, k):
+        ref = tiles.at[mine]
+        return pltpu.make_async_remote_copy(
+            src_ref=ref, dst_ref=ref, send_sem=tile_send.at[0], recv_sem=tile_recv.at[0],
+            device_id=at_group(k), device_id_type=MESH,
+        )
+
+    def send_depth_sums(count):
+        tall = jnp.zeros((NYL, NZL), f32)
+
+        def add_up(x, sums):
+            fields = [ubuf[2, x + 1, LO:HI, :]] + [bbuf[m, 2, x + 1, LO:HI, :] for m in range(count)]
+            return tuple(
+                jnp.where(lane_full == x, jnp.sum(plane, axis=1, keepdims=True), old)
+                for plane, old in zip(fields, sums)
+            )
+
+        sums = list(planes(add_up, (tall,) * (count + 1), 1)) + [tall] * (2 * across - count - 1)
+        for t in range(2):
+            square = jnp.concatenate(sums[t * across : (t + 1) * across], axis=0)
+            tiles[place, t] = jnp.transpose(square)[0:NXL]
+        for k in range(1, group):
+            tile_copy(place, k).start()
 
     def load(x, held):
         for c in range(3):
-            plane = vel[c, x]
-            ubuf[c, x + 1, LO:HI, :] = plane
-            held = pack(U_SET, c, x, plane, held)
+            for t in tiles_in:
+                held = pack(U_SET, c, x, t, ubuf[c, x + 1, at(t), :], held)
         return held
 
-    zs[U_SET] = planes(load, no_pack)
+    loads[0].wait()
+    keep_pack(U_SET, planes(load, no_pack))
     pl.semaphore_wait(barrier, px - 1 + group - 1)
     start_faces(ubuf, U_SET, 3)
 
@@ -344,6 +400,10 @@
             device_id=device, device_id_type=MESH,
         )
 
+    for copy in loads[1:]:
+        copy.wait()
+    surf[0, RIM : RIM + NXL, :] = receivers[...].astype(f32)
+    surf[1, RIM : RIM + NXL, :] = heights[...]
     for d, sends in ((0, mx < px - 1), (1, mx > 0)):
         @pl.when(sends)
         def _():
@@ -378,15 +438,16 @@
             block = pltpu.roll(block, row_step % rows, 0)
         return block
 
-    drained = jnp.ones((rows, cols), f32)
-    for _ in range(SWEEPS):
+    def sweep(_, drained):
         total = jnp.ones((rows, cols), f32)
         for direction, (row_step, col_step) in enumerate(neighbour_steps):
             chosen = code == float(direction)
             if col_step:
                 chosen = chosen & (col != (cols - 1 if col_step > 0 else 0))
             total = total + turned(jnp.where(chosen, drained, 0.0), row_step, col_step)
-        drained = total
+        return total
+
+    drained = lax.fori_loop(0, SWEEPS, sweep, jnp.ones((rows, cols), f32))
     height = surf[1]
     below = jnp.zeros((rows, cols), f32)
     spacing = jnp.ones((rows, cols), f32)
@@ -402,47 +463,53 @@
     ground = height - (surface_step * erodibility) * jnp.sqrt(drained) * slope
     base[...] = ground[RIM : RIM + NXL]
 
-    none = jnp.zeros((8, NZL), f32)
     finish_faces(ubuf, U_SET, 3)
     spread_rows(ubuf, U_SET, 3)
     for picard, count in enumerate(counts):
-        u_rim = zr[U_SET]
-
         def soften(x, held):
-            rate = rate_at(x, u_rim)
-            eta = jnp.minimum(visc[x], strength[x] / (2.0 * jnp.maximum(rate, rate_floor)))
-            ebuf[0, x + 1, LO:HI, :] = eta
-            return pack(E_SET, 0, x, eta, held)
-
-        zs[E_SET] = planes(soften, no_pack)
+            for t in tiles_in:
+                rate = rate_at(x, t)
+                eta = jnp.minimum(visc[x, own(t)], strength[x, own(t)] / (2.0 * jnp.maximum(rate, rate_floor)))
+                ebuf[0, x + 1, at(t), :] = eta
+                held = pack(E_SET, 0, x, t, eta, held)
+            return held
+
+        keep_pack(E_SET, planes(soften, no_pack))
         start_faces(ebuf, E_SET, 1)
         finish_faces(ebuf, E_SET, 1)
         spread_rows(ebuf, E_SET, 1)
-        e_rim = zr[E_SET]
         lagged = count <= CUT + 1
         gram, rows_of = {}, ([], [])
         shift = {}
 
         def begin(x, carry):
             held, norm = carry
-            eta, pairs = around(ebuf, e_rim, 0, x)
-            total = jnp.full((NYL, NZL), drag_coef, f32)
-            for d in range(3):
-                for side in range(2):
-                    face = 0.5 * (eta + pairs[d][side])
-                    coef[2 * d + side, x] = face
-                    total = total + face
-            coef[6, x] = total
-            for c in range(3):
-                _, au = applied(ubuf, u_rim, c, x)
-                plane = force[c, x] - au
-                bbuf[0, c, x + 1, LO:HI, :] = plane
-                norm = norm + fold(plane * plane)
-                held = pack(0, c, x, plane, held)
+            for t in tiles_in:
+                eta, pairs = around(ebuf, E_SET, 0, x, t)
+                total = jnp.full((8, NZL), drag_coef, f32)
+                ends = []
+                for d in range(3):
+                    for side in range(2):
+                        face = 0.5 * (eta + pairs[d][side])
+                        total = total + face
+                        if d == 2:
+                            ends.append(face)
+                            face = jnp.where(lane_tile == (NZL - 1) * side, 0.0, face)
+                        coef[2 * d + side, x, own(t)] = face
+                coef[6, x, own(t)] = total
+                coef[7, x, own(t)] = jnp.where(
+                    lane_tile == edge, jnp.where(lane_tile == 0, ends[0], ends[1]), 0.0
+                )
+                for c in range(3):
+                    _, au = applied(ubuf, U_SET, c, x, t)
+                    tile = force[c, x, own(t)] - au
+                    bbuf[0, c, x + 1, at(t), :] = tile
+                    norm = norm + tile * tile
+                    held = pack(0, c, x, t, tile, held)
             return held, norm
 
         held, norm = planes(begin, (no_pack, none), 1)
-        zs[0] = held
+        keep_pack(0, held)
         keep_dots(0, rows_of[0], [(0, 0)], [norm])
         start_faces(bbuf.at[0], 0, 3)
         early = 2 * picard
@@ -452,7 +519,6 @@
                 spread_rows(bbuf.at[k], k, 3)
             if lagged and k == CUT - 1:
                 middle_sums(early)
-            rim = zr[k]
             stored = k + 1 < count
             extra = {}
             if k >= CUT:
@@ -469,20 +535,21 @@
             def grow(x, carry):
                 held, sums = carry
                 sums = list(sums)
-                for c in range(3):
-                    v, w = applied(bbuf.at[k], rim, c, x)
-                    own = {}
-                    for m in set(extra) | set(partners):
-                        if m <= k:
-                            own[m] = v if m == k else bbuf[m, c, x + 1, LO:HI, :]
-                    for m in sorted(extra):
-                        w = w - extra[m] * own[m]
-                    own[k + 1] = w
-                    if stored:
-                        bbuf[k + 1, c, x + 1, LO:HI, :] = w
-                        held = pack(k + 1, c, x, w, held)
-                    for at, m in enumerate(partners):
-                        sums[at] = sums[at] + fold(own[m] * w)
+                for t in tiles_in:
+                    for c in range(3):
+                        v, w = applied(bbuf.at[k], k, c, x, t)
+                        mine = {}
+                        for m in sorted(set(extra) | set(partners)):
+                            if m <= k:
+                                mine[m] = v if m == k else bbuf[m, c, x + 1, at(t), :]
+                        for m in sorted(extra):
+                            w = w - extra[m] * mine[m]
+                        mine[k + 1] = w
+                        if stored:
+                            bbuf[k + 1, c, x + 1, at(t), :] = w
+                            held = pack(k + 1, c, x, t, w, held)
+                        for spot, m in enumerate(partners):
+                            sums[spot] = sums[spot] + mine[m] * w
                 return held, tuple(sums)
 
             held, sums = planes(grow, (no_pack, tuple(none for _ in partners)))
@@ -492,7 +559,7 @@
             if k + 1 == (CUT - 1 if lagged else CUT):
                 start_sums(early, 0)
             if stored:
-                zs[k + 1] = held
+                keep_pack(k + 1, held)
                 start_faces(bbuf.at[k + 1], k + 1, 3)
             if k + 1 == CUT:
                 if not lagged:
@@ -518,11 +585,12 @@
                 spread_rows(bbuf.at[CUT], CUT, 3)
 
         start_sums(early + 1, 1)
+        final = picard == len(counts) - 1
+        if final:
+            send_depth_sums(count)
         middle_sums(early + 1)
         finish_sums(early + 1, rows_of[1], gram)
         steps = solve(gram, shift, count)
-        final = picard == len(counts) - 1
-        tall = jnp.zeros((NYL, NZL), f32)
 
         def total_of(first, parts):
             for step, part in zip(steps, parts):
@@ -539,53 +607,50 @@
                 yr[U_SET, side, c] = total_of(yr[U_SET, side, c], [yr[m, side, c] for m in range(count)])
         zr[U_SET] = total_of(zr[U_SET], [zr[m] for m in range(count)])
 
-        def settle(x, sums):
+        def settle(x, _):
             for c in range(3):
-                plane = total_of(
-                    ubuf[c, x + 1, LO:HI, :], [bbuf[m, c, x + 1, LO:HI, :] for m in range(count)]
-                )
-                ubuf[c, x + 1, LO:HI, :] = plane
-                if final:
-                    vout[c, x] = plane
-                    if c == 2:
-                        sums = jnp.where(lane_full == x, jnp.sum(plane, axis=1, keepdims=True), sums)
-            return sums
-
-        sums = planes(settle, tall)
+                for t in tiles_in:
+                    tile = total_of(
+                        ubuf[c, x + 1, at(t), :], [bbuf[m, c, x + 1, at(t), :] for m in range(count)]
+                    )
+                    ubuf[c, x + 1, at(t), :] = tile
+                    if final:
+                        vout[c, x, own(t)] = tile
+            return 0
+
+        planes(settle, 0)
         spread_rows(ubuf, U_SET, 3)
 
-    square = jnp.concatenate([sums, jnp.zeros((NZL - NYL, NZL), f32)], axis=0)
-    across = NZL // NYL
-    flat = jnp.transpose(square)[0:NXL]
-    tiles[place] = pltpu.roll(flat, lax.rem(my, across) * NYL, 1)
-
-    def tile_copy(k):
-        mine = tiles.at[place]
-        return pltpu.make_async_remote_copy(
-            src_ref=mine, dst_ref=mine, send_sem=tile_send.at[k], recv_sem=tile_recv.at[k],
-            device_id=at_group(k), device_id_type=MESH,
-        )
-
-    for k in range(1, group):
-        tile_copy(k).start()
-    u_rim = zr[U_SET]
-
     def harden(x, _):
-        rate = rate_at(x, u_rim)
-        plastic = jnp.maximum(rate - strength[x] / (2.0 * visc[x]), 0.0)
-        sout[x] = strain[x] + strain_step * plastic
+        for t in tiles_in:
+            plastic = jnp.maximum(rate_at(x, t) - strength[x, own(t)] / (2.0 * visc[x, own(t)]), 0.0)
+            sout[x, own(t)] = strain[x, own(t)] + strain_step * plastic
         return 0
 
     planes(harden, 0)
-    for k in range(1, group):
-        tile_copy(k).wait()
+    tile_copy(slice(0, group - 1), 1).wait()
     scale = surface_step * uplift_gain / (pz * NZL)
+    lane_group = lax.broadcasted_iota(jnp.int32, (1, NZL), 1) // NYL
+    weights = []
+    parts = [jnp.ones((1, NZL), f32)] + steps
+    for t in range(2):
+        weight = jnp.zeros((1, NZL), f32)
+        for g, part in enumerate(parts[t * across : (t + 1) * across]):
+            weight = jnp.where(lane_group == g, scale * part, weight)
+        weights.append(weight)
+    spread_group = lanes(NXL) // NYL
     for part in range(py // across):
-        total = tiles[part * across * pz]
-        for k in range(1, across * pz):
-            total = total + tiles[part * across * pz + k]
         span = slice(part * NZL, (part + 1) * NZL)
-        tout[:, span] = base[:, span] + scale * total
+        ground = base[:, span]
+        for g in range(across):
+            total = jnp.zeros((NXL, NZL), f32)
+            for k in range(pz):
+                for t in range(2):
+                    total = total + weights[t] * tiles[(part * across + g) * pz + k, t]
+            total = total + pltpu.roll(total, NZL // 2, 1)
+            total = total + pltpu.roll(total, NYL, 1)
+            ground = ground + jnp.where(spread_group == g, total, 0.0)
+        tout[:, span] = ground
 
 
 def build(counts, ident, px, py, pz, name):
@@ -602,9 +667,16 @@
             jax.ShapeDtypeStruct(cell, f32),
             jax.ShapeDtypeStruct((NXL, cols), f32),
         ],
-        in_specs=[vmem] * 7,
+        in_specs=[pl.BlockSpec(memory_space=pl.ANY)] * 7,
         out_specs=[vmem] * 3,
         scratch_shapes=[
+            pltpu.VMEM(field, f32),
+            pltpu.VMEM(cell, f32),
+            pltpu.VMEM(cell, f32),
+            pltpu.VMEM(cell, jnp.int32),
+            pltpu.VMEM((NXL, cols), f32),
+            pltpu.VMEM((NXL, cols), jnp.int32),
+            dma((7,)),
             pltpu.VMEM((3, NXL + 2, BUFY, NZL), f32),
             pltpu.VMEM((1, NXL + 2, BUFY, NZL), f32),
             pltpu.VMEM((KMAX, 3, NXL + 2, BUFY, NZL), f32),
@@ -613,18 +685,18 @@
             pltpu.VMEM((KMAX + 2, NYL // 2, NZL), f32),
             pltpu.VMEM((KMAX + 2, NYL // 2, NZL), f32),
             pltpu.VMEM(cell, f32),
-            pltpu.VMEM((7, *cell), f32),
+            pltpu.VMEM((8, *cell), f32),
             pltpu.VMEM((2, ROWS, NZL), f32),
             pltpu.VMEM((4, px, 1, NZL), f32),
             pltpu.VMEM((4, group, 1, NZL), f32),
             pltpu.VMEM((2, NXL + 2 * RIM, cols), f32),
             pltpu.VMEM((NXL, cols), f32),
-            pltpu.VMEM((group, NXL, NZL), f32),
-            dma((KMAX + 2, 5)), dma((KMAX + 2, 5)),
-            dma((4, px)), dma((4, px)),
-            dma((4, group)), dma((4, group)),
+            pltpu.VMEM((group, 2, NXL, NZL), f32),
+            dma((5,)), dma((2, 5)),
+            dma((1,)), dma((2,)),
+            dma((1,)), dma((2,)),
             dma((2,)), dma((2,)),
-            dma((group,)), dma((group,)),
+            dma((1,)), dma((1,)),
         ],
         compiler_params=pltpu.CompilerParams(
             collective_id=ident, has_side_effects=True, vmem_limit_bytes=40 * 1024 * 1024

time: 119 us -> 112 us (0.941)
  Pallas kernels: 114 us -> 108 us
    pallas_call x1, Pallas kernels: 114 us -> 108 us  [local(): short_first(*a)]
where the time goes in v3:
time: 112 us; the launch traced here: 111 us
  Pallas kernels  108 us (96%)
  local copies, waits for them, and re-layouts  2.84 us (3%)
    pallas_call x1, Pallas kernels, local(): short_first(*a)  108 us
    unnamed x5, local copies, waits for them, and re-layouts  2.84 us

profile of v3, /device:TPU:1, one launch (start us, length us, event | category | flops | bytes accessed | tf_op | source)
XLA Modules:
  0.0 111.3 jit_solution(2652248525397132644)
XLA Ops:
  0.6 0.0 copy-start
  0.6 0.6 copy-done
  1.3 107.8 %conditional.1 = ((f32[3,16,32,128]{3,2,1,0:T(8,128)S(1)}, f32[16,32,128]{2,1,0:T(8,128)S(1)}, f32[16,256]{1,0:T(8,128)S(1)})) conditional(s32[]{:T(128)} %bitcast, (f32[3,16,32,128]{3,2,1,0:T(8,128)}, f32[3,16,32,128]{3,2,1,0:T(8,128)}, f32[16,32,128]{2,1,0:T(8,128)}, f32[16,32,128]{2,1,0:T(8,128)}, s32[16,32,128]{2,1,0:T(8,128)}, ...), branch_computations={%region_0.0_spmd, %region_1.0_spmd} | conditional | bytes 8 | solution.py:712
  1.3 107.8 %short_first.1 = (f32[3,16,32,128]{3,2,1,0:T(8,128)S(1)}, f32[16,32,128]{2,1,0:T(8,128)S(1)}, f32[16,256]{1,0:T(8,128)S(1)}) custom-call(f32[3,16,32,128]{3,2,1,0:T(8,128)} %get-tuple-element.28.force_in, f32[3,16,32,128]{3,2,1,0:T(8,128)} %get-tuple-element.29.vel_in, f32[16,32,128]{2,1,0:T(8,128)} %get-tuple-element.30.visc_in, ...), custom_call_target="tpu_custom_call" | custom-call | tf_op jit(solution)/shard_map/cond/branch_0_fun/short_first/pallas_call | solution.py:712
  109.1 0.9 copy.26
  110.0 0.7 copy.27
  110.7 0.6 copy.28
Async XLA Ops:
  0.6 0.7 copy-start

commit v4 on v3

--- a/solution.py
+++ b/solution.py
@@ -277,7 +277,7 @@
             total = total + 0.5 * (shear * shear)
         return jnp.sqrt(0.5 * total)
 
-    def planes(body, carry, unroll=2):
+    def planes(body, carry, unroll=4):
         return lax.fori_loop(0, NXL, body, carry, unroll=unroll)
 
     def sum_copy(sums, slot, mine, send, recv, device):
@@ -376,6 +376,8 @@
         for t in range(2):
             square = jnp.concatenate(sums[t * across : (t + 1) * across], axis=0)
             tiles[place, t] = jnp.transpose(square)[0:NXL]
+
+    def start_tiles():
         for k in range(1, group):
             tile_copy(place, k).start()
 
@@ -547,12 +549,19 @@
                         mine[k + 1] = w
                         if stored:
                             bbuf[k + 1, c, x + 1, at(t), :] = w
-                            held = pack(k + 1, c, x, t, w, held)
                         for spot, m in enumerate(partners):
                             sums[spot] = sums[spot] + mine[m] * w
                 return held, tuple(sums)
 
             held, sums = planes(grow, (no_pack, tuple(none for _ in partners)))
+            if stored:
+                def wrap(x, held):
+                    for c in range(3):
+                        for t in tiles_in:
+                            held = pack(k + 1, c, x, t, bbuf[k + 1, c, x + 1, at(t), :], held)
+                    return held
+
+                held = planes(wrap, held, 4)
             shift[k] = dict(extra)
             bank = 0 if k + 1 < CUT or (k + 1 == CUT and not lagged) else 1
             keep_dots(bank, rows_of[bank], [(m, k + 1) for m in partners], sums)
@@ -589,6 +598,8 @@
         if final:
             send_depth_sums(count)
         middle_sums(early + 1)
+        if final:
+            start_tiles()
         finish_sums(early + 1, rows_of[1], gram)
         steps = solve(gram, shift, count)
 

time: 112 us -> 106 us (0.946)
  Pallas kernels: 108 us -> 103 us
    pallas_call x1, Pallas kernels: 108 us -> 103 us  [local(): short_first(*a)]
where the time goes in v4:
time: 106 us
  Pallas kernels  103 us (97%)
  local copies, waits for them, and re-layouts  2.84 us (3%)
    pallas_call x1, Pallas kernels, local(): short_first(*a)  103 us
    unnamed x5, local copies, waits for them, and re-layouts  2.84 us

profile of v4, /device:TPU:1, one launch (start us, length us, event | category | flops | bytes accessed | tf_op | source)
XLA Modules:
  0.0 106.3 jit_solution(6921833228179437403)
XLA Ops:
  0.6 0.0 copy-start
  0.6 0.6 copy-done
  1.3 102.8 %conditional.1 = ((f32[3,16,32,128]{3,2,1,0:T(8,128)S(1)}, f32[16,32,128]{2,1,0:T(8,128)S(1)}, f32[16,256]{1,0:T(8,128)S(1)})) conditional(s32[]{:T(128)} %bitcast, (f32[3,16,32,128]{3,2,1,0:T(8,128)}, f32[3,16,32,128]{3,2,1,0:T(8,128)}, f32[16,32,128]{2,1,0:T(8,128)}, f32[16,32,128]{2,1,0:T(8,128)}, s32[16,32,128]{2,1,0:T(8,128)}, ...), branch_computations={%region_0.0_spmd, %region_1.0_spmd} | conditional | bytes 8 | solution.py:723
  1.3 102.6 %short_first.1 = (f32[3,16,32,128]{3,2,1,0:T(8,128)S(1)}, f32[16,32,128]{2,1,0:T(8,128)S(1)}, f32[16,256]{1,0:T(8,128)S(1)}) custom-call(f32[3,16,32,128]{3,2,1,0:T(8,128)} %get-tuple-element.28.force_in, f32[3,16,32,128]{3,2,1,0:T(8,128)} %get-tuple-element.29.vel_in, f32[16,32,128]{2,1,0:T(8,128)} %get-tuple-element.30.visc_in, ...), custom_call_target="tpu_custom_call" | custom-call | tf_op jit(solution)/shard_map/cond/branch_0_fun/short_first/pallas_call | solution.py:723
  104.1 0.9 copy.26
  105.0 0.7 copy.27
  105.7 0.6 copy.28
Async XLA Ops:
  0.6 0.7 copy-start
